TPU v7x, 256 devices: a whole 4x4x8 slice. The times are simulated.
256 devices in a mesh: frame: 8 (over z_hi, x), tile: 32 (over y, z_lo, core).
Axes of the slice: x: 4, y: 4, z: 8 (z_hi: 2, z_lo: 4; z = z_hi * 4 + z_lo), core: 2. Of those that a mesh axis runs over, the one named last changes fastest.
Arguments:
- latents: bfloat16 [16, 128, 128, 512], P('frame', 'tile'), may hold values from -6 to 6
- conv_weight: bfloat16 [3, 3, 512, 512], replicated, may hold values from -0.09375 to 0.09375
- conv_bias: float32 [512], replicated, may hold values from -3 to 3
- query_weight: bfloat16 [512, 512], replicated, may hold values from -0.176776695 to 0.176776695
- key_weight: bfloat16 [512, 512], replicated, may hold values from -8 to 8
- value_weight: bfloat16 [512, 512], replicated, may hold values from -0.25 to 0.25
- out_weight: bfloat16 [512, 512], replicated, may hold values from -0.25 to 0.25
- cotangent: bfloat16 [16, 128, 128, 512], P('frame', 'tile'), may hold values from -0.01171875 to 0.01171875
Outputs:
- mixed_frames: bfloat16 [16, 128, 128, 512], P('frame', 'tile')
- conv_grad: float32 [512, 4608], P('tile', 'frame')
All inputs are finite; a program needn't handle non-finite values.
Results may differ from a plain program's by a relative error of at most 0.0065.
Values may be sent and summed in bfloat16 or wider, within the bound.
No kernel may reach another device: no remote copies, remote signals or barrier semaphores. Data moves between devices by JAX's collectives and lax.ppermute only.
A program may use at most 128 MiB of HBM per device.

v0:
```python
import math

import jax
import jax.numpy as jnp
from jax import lax
from jax.sharding import Mesh
from jax.sharding import PartitionSpec as P

HEADS = 8
TILE = ("tile_0", "tile_1", "tile_2")


def with_halo(cells, sides, width):
    for axis, dim in sides:
        count = lax.axis_size(axis)
        ends = count - 1
        head = lax.slice_in_dim(cells, 0, width, axis=dim)
        tail = lax.slice_in_dim(cells, cells.shape[dim] - width, cells.shape[dim], axis=dim)
        cells = jnp.concatenate(
            [
                lax.ppermute(tail, axis, [(i, (i + 1) % count) for i in range(ends)]),
                cells,
                lax.ppermute(head, axis, [((i + 1) % count, i) for i in range(ends)]),
            ],
            axis=dim,
        )
    return cells


def cut_along(value, dim, length):
    before, after = (value.shape[:dim], value.shape[dim + 1 :])
    return jnp.moveaxis(value.reshape(*before, length, -1, *after), dim, 0)


def sum_by_chip(value, chips, core, dim):
    sizes = (lax.axis_size(chips), lax.axis_size(core))
    parts = cut_along(value, dim, sizes[0] * sizes[1])
    inside = parts.shape[1:]
    parts = parts.reshape(*sizes, *inside).swapaxes(0, 1).reshape(-1, *inside)
    parts = lax.psum_scatter(parts, core, scatter_dimension=0, tiled=True)
    return lax.psum_scatter(parts, chips, scatter_dimension=0, tiled=True)[0]


def sum_at_owner(value, axis, dim):
    length = lax.axis_size(axis)
    parts = lax.all_to_all(cut_along(value, dim, length), axis, 0, 0, tiled=True)
    return jnp.sum(parts, axis=0)


def on_device(
    latents, conv_weight, conv_bias, query_weight, key_weight, value_weight, out_weight, cotangent
):
    channels = latents.shape[3]
    head_dim = channels // HEADS
    padded = with_halo(latents, ((TILE, 1),), 1)
    convolved = lax.conv_general_dilated(
        padded,
        conv_weight,
        (1, 1),
        ((0, 0), (1, 1)),
        dimension_numbers=("NHWC", "HWIO", "NHWC"),
        preferred_element_type=jnp.float32,
    )
    hidden = jax.nn.silu(convolved + conv_bias).astype(jnp.bfloat16)
    blocked = lax.all_to_all(hidden, "frame", split_axis=2, concat_axis=0, tiled=True)
    frames, row_count, col_count, _ = blocked.shape
    tokens = blocked.reshape(-1, channels)
    queries = jnp.dot(tokens, query_weight, preferred_element_type=jnp.float32).astype(jnp.bfloat16)
    key_rows = jnp.dot(tokens, key_weight, preferred_element_type=jnp.float32).astype(jnp.bfloat16)
    values = jnp.dot(tokens, value_weight, preferred_element_type=jnp.float32).astype(jnp.bfloat16)
    shaped = (frames, row_count * col_count, HEADS, head_dim)
    queries = queries.reshape(shaped)
    key_rows = key_rows.reshape(shaped)
    values = values.reshape(shaped)
    scores = jnp.einsum(
        "fphd,gphd->phfg", queries, key_rows, preferred_element_type=jnp.float32
    ) / math.sqrt(head_dim)
    weights = jax.nn.softmax(scores, axis=-1).astype(jnp.bfloat16)
    head_out = jnp.einsum(
        "phfg,gphd->fphd", weights, values, preferred_element_type=jnp.float32
    ).astype(jnp.bfloat16)
    projected = jnp.dot(
        head_out.reshape(-1, channels), out_weight, preferred_element_type=jnp.float32
    )
    mixed_tokens = tokens.astype(jnp.float32) + projected
    pixel_mixed = mixed_tokens.astype(jnp.bfloat16).reshape(frames, row_count, col_count, channels)
    mixed_frames = lax.all_to_all(pixel_mixed, "frame", split_axis=0, concat_axis=2, tiled=True)
    rimmed = with_halo(mixed_frames, ((TILE, 1),), 1)
    widened = jnp.pad(rimmed, ((0, 0), (0, 0), (1, 1), (0, 0)))
    row_count = mixed_frames.shape[1]
    col_count = mixed_frames.shape[2]
    pieces = []
    for row_shift in range(3):
        for col_shift in range(3):
            pieces.append(
                widened[
                    :, row_shift : row_shift + row_count, col_shift : col_shift + col_count, :
                ].reshape(-1, channels)
            )
    patches = jnp.concatenate(pieces, axis=1)
    flat_cot = cotangent.reshape(-1, channels)
    partial_grad = sum_by_chip(
        lax.dot_general(
            flat_cot, patches, (((0,), (0,)), ((), ())), preferred_element_type=jnp.float32
        ),
        ("tile_0", "tile_1"),
        "tile_2",
        0,
    )
    conv_grad = sum_at_owner(partial_grad, "frame", 1)
    return (mixed_frames, conv_grad)


def solution(mesh):
    split = Mesh(
        mesh.devices.reshape(mesh.shape["frame"], 4, 4, 2), ("frame", "tile_0", "tile_1", "tile_2")
    )
    in_specs = (
        P("frame", TILE, None, None),
        P(),
        P(),
        P(),
        P(),
        P(),
        P(),
        P("frame", TILE, None, None),
    )
    out_specs = (P("frame", TILE, None, None), P(TILE, "frame"))
    return jax.shard_map(
        on_device, mesh=split, in_specs=in_specs, out_specs=out_specs, check_vma=False
    )
```

profile of v0, /device:TPU:8, one launch (start us, length us, event | category | flops | bytes accessed | tf_op | source)
XLA Modules:
  0.0 328.8 jit_solution(10351193222289289607)
XLA Ops:
  8.5 2.1 collective-permute-start
  10.5 6.3 %collective-permute-start.1 = (bf16[2,1,128,512]{3,2,1,0:T(8,128)(2,1)S(1)}, bf16[2,1,128,512]{3,2,1,0:T(8,128)(2,1)S(1)}, u32[]{:S(2)}, u32[]{:S(2)}) collective-permute-start(bf16[2,1,128,512]{3,2,1,0:T(8,128)(2,1)S(1)} %get-tuple-element.13), channel_id=1, source_target_pairs={{1,0},{2,1},{3,2},{4,3},{5,4},{6,5},{7,6},{8,7},{9,8},{10,9},{11,1... | collective-permute-start | bytes 786440 | tf_op jit(solution)/shard_map/ppermute | solution.py:23
  16.9 2.2 collective-permute-done
  27.0 5.8 %multiply_convert_fusion = bf16[4,16,17,512]{3,1,2,0:T(8,128)(2,1)S(1)} fusion(bf16[3,3,512,512]{3,2,1,0:T(8,128)(2,1)S(1)} %bitcast.83, bf16[6,2,8,19,512]{4,1,3,2,0:T(2,128)(2,1)S(1)} %fusion.17, f32[512]{0:T(512)S(1)} %copy-done.7, pred[16,17]{0,1:T(8,128)(4,1)S(1)} %copy-done.8), kind=kOutput, calls=%fused_computation.9 | convolution fusion | flops 5137727488 | bytes 7702800 | tf_op jit(solution)/shard_map/conv_general_dilated | solution.py:56
  34.3 38.9 %all_to_all.38 = bf16[2,4,128,512]{3,1,0,2:T(4,128)(2,1)S(1)} all-to-all(bf16[2,4,128,512]{3,1,0,2:T(4,128)(2,1)S(1)} %copy.32), channel_id=1, replica_groups=mesh['frame'=8,'tile_0'=4,'tile_1'=4,'tile_2'=2] {'frame'}, dimensions={2} | all-to-all | bytes 2097152 | tf_op jit(solution)/shard_map/all_to_all | solution.py:65
  76.3 2.8 reshape.63
  79.1 3.0 convolution_convert_fusion.1
  82.1 3.9 %reshape.62 = bf16[16,64,8,64]{3,2,1,0:T(8,128)(2,1)} reshape(bf16[1024,512]{1,0:T(8,128)(2,1)} %convolution_convert_fusion.1) | data formatting | bytes 2097152 | tf_op jit(solution)/shard_map/reshape | solution.py:72
  86.0 4.1 %fusion.7 = f32[64,8,16,16]{2,3,1,0:T(8,128)S(1)} fusion(bf16[16,64,8,64]{3,2,1,0:T(8,128)(2,1)S(1)} %reshape.63, bf16[16,64,8,64]{3,2,1,0:T(8,128)(2,1)} %reshape.62), kind=kOutput, calls=%fused_computation.12 | convolution fusion | flops 16777216 | bytes 2621440 | tf_op jit(solution)/shard_map/fphd,gphd->phfg/dot_general | solution.py:75
  90.1 3.4 %fusion.29 = (f32[64,8,16]{2,1,0:T(8,128)S(1)}, f32[64,8,16,16]{2,3,1,0:T(8,128)}) fusion(f32[64,8,16,16]{2,3,1,0:T(8,128)S(1)} %fusion.7), kind=kOutput, calls=%fused_computation.49 | output fusion | flops 524303 | bytes 1081344 | tf_op jit(solution)/shard_map/sub | solution.py:78
  95.2 2.8 reshape.61
  98.0 3.8 %convert_bitcast_fusion = bf16[16,64,8,64]{3,0,2,1:T(8,128)(2,1)S(1)} fusion(f32[64,8,16,16]{2,3,1,0:T(8,128)} %get-tuple-element.15, f32[64,8,16]{2,1,0:T(8,128)S(1)} %get-tuple-element.14, bf16[16,64,8,64]{3,2,1,0:T(8,128)(2,1)S(1)} %reshape.61), kind=kOutput, calls=%fused_computation.16 | convolution fusion | flops 17563648 | bytes 2654208 | tf_op jit(solution)/shard_map/phfg,gphd->fphd/dot_general | solution.py:79
  102.4 2.0 reshape.64
  104.4 2.4 add_convert_fusion
  106.8 29.7 %all_to_all.39 = bf16[16,4,16,512]{3,2,1,0:T(8,128)(2,1)S(1)} all-to-all(bf16[16,4,16,512]{3,2,1,0:T(8,128)(2,1)S(1)} %bitcast.81), channel_id=1, replica_groups=mesh['frame'=8,'tile_0'=4,'tile_1'=4,'tile_2'=2] {'frame'}, dimensions={0} | all-to-all | bytes 2097152 | tf_op jit(solution)/shard_map/all_to_all | solution.py:87
  136.7 1.9 collective-permute-start.2
  138.6 6.3 %collective-permute-start.3 = (bf16[2,1,128,512]{3,2,1,0:T(8,128)(2,1)S(1)}, bf16[2,1,128,512]{3,2,1,0:T(8,128)(2,1)S(1)}, u32[]{:S(2)}, u32[]{:S(2)}) collective-permute-start(bf16[2,1,128,512]{3,2,1,0:T(8,128)(2,1)S(1)} %get-tuple-element.11), channel_id=1, source_target_pairs={{1,0},{2,1},{3,2},{4,3},{5,4},{6,5},{7,6},{8,7},{9,8},{10,9},{11,1... | collective-permute-start | bytes 786440 | tf_op jit(solution)/shard_map/ppermute | solution.py:23
  144.9 2.2 collective-permute-done.2
  151.1 3.6 %copy-done.4 = bf16[1024,4608]{1,0:T(8,128)(2,1)} copy-done((bf16[1024,4608]{1,0:T(8,128)(2,1)}, bf16[1024,4608]{1,0:T(8,128)(2,1)S(1)}, u32[]{:S(2)}) %copy-start.4) | copy-done | bytes 9437208
  154.7 7.9 %fusion.30 = f32[4608,512]{0,1:T(8,128)S(1)} fusion(bf16[1024,4608]{1,0:T(8,128)(2,1)} %copy-done.4, bf16[1024,512]{1,0:T(8,128)(2,1)S(1)} %bitcast.55), kind=kOutput, calls=%fused_computation.50 | convolution fusion | flops 4831838208 | bytes 19922944 | tf_op jit(solution)/shard_map/dot_general | solution.py:103
  162.6 4.3 %copy.41 = f32[16,2,16,4608]{3,2,0,1:T(8,128)} copy(f32[16,2,16,4608]{3,2,1,0:T(8,128)S(1)} %bitcast.62) | data formatting | bytes 18874368 | tf_op jit(solution)/shard_map/reshape;reshape | solution.py:39
  167.0 18.5 %reduce-scatter.3.cloned.1.call-done = f32[16,16,4608]{2,1,0:T(8,128)} async-done(((f32[32,16,4608]{2,1,0:T(8,128)}), f32[16,16,4608]{2,1,0:T(8,128)}) %reduce-scatter.3.cloned.1.call-update) | async-done | bytes 4718608 | tf_op jit(solution)/shard_map/reduce_scatter | solution.py:40
  185.5 114.3 %reduce-scatter.5.cloned.1.call-done = f32[1,16,4608]{2,1,0:T(8,128)} async-done(((f32[16,16,4608]{2,1,0:T(8,128)}), f32[1,16,4608]{2,1,0:T(8,128)}) %reduce-scatter.5.cloned.1.call-update) | async-done | bytes 294928 | tf_op jit(solution)/shard_map/reduce_scatter | solution.py:41
  300.9 20.4 %all_to_all.40 = f32[8,16,576]{2,1,0:T(8,128)S(1)} all-to-all(f32[8,16,576]{2,1,0:T(8,128)S(1)} %bitcast.76), channel_id=1, replica_groups=mesh['frame'=8,'tile_0'=4,'tile_1'=4,'tile_2'=2] {'frame'}, dimensions={0} | all-to-all | bytes 589824 | tf_op jit(solution)/shard_map/all_to_all | solution.py:46
  (59 shorter events, 21.7 us)
Async XLA Ops:
  7.2 147.6 %copy-start = (bf16[2,4,128,512]{3,2,1,0:T(8,128)(2,1)S(1)}, bf16[2,4,128,512]{3,2,1,0:T(8,128)(2,1)}, u32[]{:S(2)}) copy-start(bf16[2,4,128,512]{3,2,1,0:T(8,128)(2,1)} %param.15) | copy-start | bytes 3145732
  7.2 178.3 %reduce-scatter.3.cloned.1.call-start = ((), (), s32[]{:S(2)}) async-start(), calls=%async_computation.5 | async-start | bytes 14155776 | tf_op jit(solution)/shard_map/reduce_scatter | solution.py:40
  7.2 19.7 %slice-start = ((s8[4718592]{0:T(1024)(128)(4,1)}), s8[4194304]{0:T(1024)(128)(4,1)S(1)}, s32[]{:S(2)}) async-start(s8[4718592]{0:T(1024)(128)(4,1)} %bitcast.82), calls=%async_computation.7 | async-start | bytes 8388608
  8.5 10.6 %collective-permute-start = (bf16[2,1,128,512]{3,2,1,0:T(8,128)(2,1)S(1)}, bf16[2,1,128,512]{3,2,1,0:T(8,128)(2,1)S(1)}, u32[]{:S(2)}, u32[]{:S(2)}) collective-permute-start(bf16[2,1,128,512]{3,2,1,0:T(8,128)(2,1)S(1)} %get-tuple-element.12), channel_id=1, source_target_pairs={{0,1},{1,2},{2,3},{3,4},{4,5},{5,6},{6,7},{7,8},{8,9},{9,10},{10,1... | collective-permute-start | bytes 786440 | tf_op jit(solution)/shard_map/ppermute | solution.py:21
  10.5 10.2 %collective-permute-start.1 = (bf16[2,1,128,512]{3,2,1,0:T(8,128)(2,1)S(1)}, bf16[2,1,128,512]{3,2,1,0:T(8,128)(2,1)S(1)}, u32[]{:S(2)}, u32[]{:S(2)}) collective-permute-start(bf16[2,1,128,512]{3,2,1,0:T(8,128)(2,1)S(1)} %get-tuple-element.13), channel_id=1, source_target_pairs={{1,0},{2,1},{3,2},{4,3},{5,4},{6,5},{7,6},{8,7},{9,8},{10,9},{11,1... | collective-permute-start | bytes 786440 | tf_op jit(solution)/shard_map/ppermute | solution.py:23
  22.2 4.8 %slice-start.1 = ((s8[4718592]{0:T(1024)(128)(4,1)}), s8[524288]{0:T(1024)(128)(4,1)S(1)}, s32[]{:S(2)}) async-start(s8[4718592]{0:T(1024)(128)(4,1)} %bitcast.82), calls=%async_computation.8 | async-start | bytes 1048576
  25.1 1.9 copy-start.7
  25.1 1.9 copy-start.8
  73.2 1.4 copy-start.5
  73.6 1.0 copy-start.2
  90.1 3.4 %copy-start.3 = (bf16[8,2,4,16,512]{4,3,2,1,0:T(8,128)(2,1)S(1)}, bf16[8,2,4,16,512]{4,3,2,1,0:T(8,128)(2,1)}, u32[]{:S(2)}) copy-start(bf16[8,2,4,16,512]{4,3,2,1,0:T(8,128)(2,1)} %copy-done.2) | copy-start | bytes 3145732
  90.1 3.4 %copy-start.6 = (bf16[512,512]{1,0:T(8,128)(2,1)S(1)}, bf16[512,512]{1,0:T(8,128)(2,1)}, u32[]{:S(2)}) copy-start(bf16[512,512]{1,0:T(8,128)(2,1)} %param.13) | copy-start | bytes 1572868
  136.6 14.1 %copy-start.1 = (bf16[8,2,4,16,512]{4,3,0,2,1:T(8,128)(2,1)}, bf16[8,2,4,16,512]{4,3,0,2,1:T(8,128)(2,1)S(1)}, u32[]{:S(2)}) copy-start(bf16[8,2,4,16,512]{4,3,0,2,1:T(8,128)(2,1)S(1)} %copy.40) | copy-start | bytes 3145732
  136.7 10.5 %collective-permute-start.2 = (bf16[2,1,128,512]{3,2,1,0:T(8,128)(2,1)S(1)}, bf16[2,1,128,512]{3,2,1,0:T(8,128)(2,1)S(1)}, u32[]{:S(2)}, u32[]{:S(2)}) collective-permute-start(bf16[2,1,128,512]{3,2,1,0:T(8,128)(2,1)S(1)} %get-tuple-element.10), channel_id=1, source_target_pairs={{0,1},{1,2},{2,3},{3,4},{4,5},{5,6},{6,7},{7,8},{8,9},{9,10},{10,1... | collective-permute-start | bytes 786440 | tf_op jit(solution)/shard_map/ppermute | solution.py:21
  138.6 10.2 %collective-permute-start.3 = (bf16[2,1,128,512]{3,2,1,0:T(8,128)(2,1)S(1)}, bf16[2,1,128,512]{3,2,1,0:T(8,128)(2,1)S(1)}, u32[]{:S(2)}, u32[]{:S(2)}) collective-permute-start(bf16[2,1,128,512]{3,2,1,0:T(8,128)(2,1)S(1)} %get-tuple-element.11), channel_id=1, source_target_pairs={{1,0},{2,1},{3,2},{4,3},{5,4},{6,5},{7,6},{8,7},{9,8},{10,9},{11,1... | collective-permute-start | bytes 786440 | tf_op jit(solution)/shard_map/ppermute | solution.py:23
  151.1 3.6 %copy-start.4 = (bf16[1024,4608]{1,0:T(8,128)(2,1)}, bf16[1024,4608]{1,0:T(8,128)(2,1)S(1)}, u32[]{:S(2)}) copy-start(bf16[1024,4608]{1,0:T(8,128)(2,1)S(1)} %constant_dynamic-update-slice_fusion) | copy-start | bytes 28311556
  166.9 132.9 %reduce-scatter.5.cloned.1.call-start = ((), (), s32[]{:S(2)}) async-start(), calls=%async_computation.6 | async-start | bytes 5013504 | tf_op jit(solution)/shard_map/reduce_scatter | solution.py:41
Sparse Core Ops, SparseCore 0:
  167.0 18.3 reduce-scatter.2
  188.0 111.6 reduce-scatter.4
where the time goes:
time: 329 us
  waiting for transfers between devices  141 us (43%)
  blocking collectives  89 us (27%)
  matrix products  30.3 us (9%)
  local copies, waits for them, and re-layouts  30 us (9%)
  starting transfers between devices  16.7 us (5%)
  between operations  14.4 us (4%)
  other arithmetic  7.79 us (2%)
    reduce_scatter x1, waiting for transfers between devices, sum_by_chip(): return lax.psum_scatter(parts, chips, scatter_dimension=0, tiled=True)[0]  114 us
    all_to_all x1, blocking collectives, on_device(): lax.all_to_all(hidden, 'frame', split_axis=2, concat_axis=0, tiled=True)  38.9 us
    all_to_all x1, blocking collectives, on_device(): lax.all_to_all(pixel_mixed, 'frame', split_axis=0, concat_axis=2, tiled=T...  29.7 us
    all_to_all x1, blocking collectives, sum_at_owner(): lax.all_to_all(cut_along(value, dim, length), axis, 0, 0, tiled=True)  20.4 us
    reduce_scatter x1, waiting for transfers between devices, sum_by_chip(): parts = lax.psum_scatter(parts, core, scatter_dimension=0, tiled=True)  18.5 us
    ppermute x2, starting transfers between devices, with_halo(): lax.ppermute(head, axis, [((i + 1) % count, i) for i in range(ends)])  12.7 us
    dot_general x1, matrix products, on_device(): lax.dot_general(flat_cot, patches, (((0,), (0,)), ((), ())), preferred_el...  7.87 us
    unnamed x31, local copies, waits for them, and re-layouts  6.84 us
  transfers between devices with their start and end apart: 6, of which 6 were waited for; matrix products, arithmetic and copies ran while one was open for 0% of the time, Pallas kernels for 0%

commit v1 on v0

v1 whole, which is shorter than its diff:
```python
import math

import jax
import jax.numpy as jnp
from jax import lax
from jax.experimental import pallas as pl
from jax.experimental.pallas import tpu as pltpu
from jax.sharding import Mesh
from jax.sharding import PartitionSpec as P


HEADS = 8
FRAME = ("zh", "x")
TILE = ("y", "zl", "core")
F32 = jnp.float32
BF16 = jnp.bfloat16


def edge_rows(cells):
    count = math.prod(lax.axis_size(a) for a in TILE)
    head = cells[:, :1]
    tail = cells[:, -1:]
    above = lax.ppermute(tail, TILE, [(i, i + 1) for i in range(count - 1)])
    below = lax.ppermute(head, TILE, [(i + 1, i) for i in range(count - 1)])
    return above, below


def conv_kernel(above_ref, own_ref, below_ref, weight_ref, bias_ref, out_ref, rows_ref, acc_ref):
    s = pl.program_id(0)
    frames, height, cols, channels = own_ref.shape
    pixels = height * cols

    @pl.when(s == 0)
    def _():
        for f in range(frames):
            rows_ref[f, :cols] = above_ref[f, 0]
            rows_ref[f, cols : cols + pixels] = own_ref[f].reshape(pixels, channels)
            rows_ref[f, cols + pixels :] = below_ref[f, 0]

    column = lax.broadcasted_iota(jnp.int32, (pixels, 1), 0) % cols
    blocks = out_ref.shape[0]
    for f in range(frames):
        part = None
        for r in range(3):
            term = jnp.dot(
                rows_ref[f, r * cols : r * cols + pixels],
                weight_ref[r, 0],
                preferred_element_type=F32,
            )
            part = term if part is None else part + term

        @pl.when(s == 0)
        def _():
            acc_ref[f] = jnp.where(column > 0, pltpu.roll(part, 1, 0), 0.0)

        @pl.when(s == 1)
        def _():
            acc_ref[f] += part

        @pl.when(s == 2)
        def _():
            moved = jnp.where(column < cols - 1, pltpu.roll(part, pixels - 1, 0), 0.0)
            v = acc_ref[f] + moved + bias_ref[...]
            h = (v / (1.0 + jnp.exp(-v))).astype(BF16)
            h = h.reshape(height, blocks, cols // blocks, channels)
            for b in range(blocks):
                out_ref[b, f] = h[:, b]


def conv_silu(above, own, below, weight, bias, blocks):
    frames, height, cols, channels = own.shape
    edge = pl.BlockSpec(above.shape, lambda s: (0, 0, 0, 0))
    out_shape = (blocks, frames, height, cols // blocks, channels)
    return pl.pallas_call(
        conv_kernel,
        grid=(3,),
        in_specs=[
            edge,
            pl.BlockSpec(own.shape, lambda s: (0, 0, 0, 0)),
            edge,
            pl.BlockSpec((3, 1, channels, channels), lambda s: (0, s, 0, 0)),
            pl.BlockSpec((1, channels), lambda s: (0, 0)),
        ],
        out_specs=pl.BlockSpec(out_shape, lambda s: (0, 0, 0, 0, 0)),
        out_shape=jax.ShapeDtypeStruct(out_shape, BF16),
        scratch_shapes=[
            pltpu.VMEM((frames, (height + 2) * cols, channels), BF16),
            pltpu.VMEM((frames, height * cols, channels), F32),
        ],
        cost_estimate=pl.CostEstimate(flops=5 * 10**9, bytes_accessed=8 * 10**6, transcendentals=0),
        name="conv_silu",
    )(above, own, below, weight, bias.reshape(1, channels))


def attention_kernel(x_ref, wqkv_ref, wo_ref, out_ref):
    frames, _, cols, channels = x_ref.shape
    tokens = frames * cols
    x = x_ref[...].reshape(tokens, channels)
    qkv = jnp.dot(x, wqkv_ref[...], preferred_element_type=F32).astype(BF16)
    pair = 2 * (channels // HEADS)
    row = lax.broadcasted_iota(jnp.int32, (tokens, tokens), 0)
    col = lax.broadcasted_iota(jnp.int32, (tokens, tokens), 1)
    same = (row % cols) == (col % cols)
    lane = lax.broadcasted_iota(jnp.int32, (tokens, pair), 1)
    first = lane < pair // 2
    one = jnp.ones((tokens, pair), F32).astype(BF16)
    zero = jnp.zeros((tokens, pair), F32).astype(BF16)
    scale = math.log2(math.e) / math.sqrt(channels // HEADS)
    outs = []
    for p in range(HEADS // 2):
        lo = p * pair
        q = qkv[:, lo : lo + pair]
        k = qkv[:, channels + lo : channels + lo + pair]
        v = qkv[:, 2 * channels + lo : 2 * channels + lo + pair]
        total = None
        for half in range(2):
            keep = first if half == 0 else jnp.logical_not(first)
            k_half = jnp.where(keep, k, zero)
            s = lax.dot_general(q, k_half, (((1,), (1,)), ((), ())), preferred_element_type=F32)
            s = jnp.where(same, s, -1e30)
            m = jnp.max(s, axis=1, keepdims=True)
            e = jnp.exp2((s - m) * scale).astype(BF16)
            rhs = jnp.concatenate([jnp.where(keep, v, zero), jnp.where(keep, one, zero)], axis=1)
            part = jnp.dot(e, rhs, preferred_element_type=F32)
            total = part if total is None else total + part
        outs.append((total[:, :pair] / total[:, pair:]).astype(BF16))
    head_out = jnp.concatenate(outs, axis=1)
    mixed = x.astype(F32) + jnp.dot(head_out, wo_ref[...], preferred_element_type=F32)
    out_ref[...] = mixed.astype(BF16).reshape(out_ref.shape)


def attend(blocked, wqkv, wo):
    frames, rows, cols, channels = blocked.shape
    spec = pl.BlockSpec((frames, 1, cols, channels), lambda r: (0, r, 0, 0))
    return pl.pallas_call(
        attention_kernel,
        grid=(rows,),
        in_specs=[
            spec,
            pl.BlockSpec(wqkv.shape, lambda r: (0, 0)),
            pl.BlockSpec(wo.shape, lambda r: (0, 0)),
        ],
        out_specs=spec,
        out_shape=jax.ShapeDtypeStruct(blocked.shape, BF16),
        cost_estimate=pl.CostEstimate(flops=5 * 10**9, bytes_accessed=4 * 10**6, transcendentals=0),
        name="attend",
    )(blocked, wqkv, wo)


def grad_kernel(*refs):
    cots, mixes, out_ref = (refs[:3], refs[3:6]), refs[6:8], refs[8]
    r = pl.program_id(0)
    blocks, frames, height, width, channels = mixes[0].shape
    cols = blocks * width
    pixels = height * cols
    outs = cots[0][0].shape[0]
    acc = None
    for side in range(2):
        for f in range(frames):
            mix = jnp.concatenate(
                [mixes[side][b, f, y] for y in range(height) for b in range(blocks)], axis=0
            )
            start = pl.multiple_of(f * (pixels + 2 * cols) + (2 - r) * cols, cols)
            cot = jnp.concatenate([c[:, pl.ds(start, pixels)] for c in cots[side]], axis=0)
            part = jnp.dot(cot, mix, preferred_element_type=F32)
            acc = part if acc is None else acc + part
    flat = jnp.concatenate([acc[s * outs : (s + 1) * outs] for s in range(3)], axis=1).astype(BF16)
    places = out_ref.shape[0]
    block = channels * 9 // (2 * places)
    for step in range(3):

        @pl.when(r == step)
        def _():
            lo = step * 3 * channels
            for k in range(2 * places):
                a, b = max(lo, k * block), min(lo + 3 * channels, (k + 1) * block)
                if a < b:
                    to = (k // places) * block + a - k * block
                    out_ref[k % places, :, to : to + b - a] = flat[:, a - lo : b - lo]


def kernel_grad(cots, mixes, places):
    outs, width = cots[0].shape
    channels = mixes[0].shape[-1]
    out_shape = (places, outs, 9 * channels // places)
    cot_spec = pl.BlockSpec((outs, width), lambda r: (0, 0))
    mix_spec = pl.BlockSpec(mixes[0].shape, lambda r: (0, 0, 0, 0, 0))
    return pl.pallas_call(
        grad_kernel,
        grid=(3,),
        in_specs=[cot_spec] * 6 + [mix_spec] * 2,
        out_specs=pl.BlockSpec(out_shape, lambda r: (0, 0, 0)),
        out_shape=jax.ShapeDtypeStruct(out_shape, BF16),
        cost_estimate=pl.CostEstimate(flops=5 * 10**9, bytes_accessed=8 * 10**6, transcendentals=0),
        name="kernel_grad",
    )(*cots, *mixes)


def swap_core(value):
    return lax.ppermute(value, "core", [(0, 1), (1, 0)])


def shifted_cotangent(cotangent, above, below):
    rim = jnp.concatenate([above, cotangent, below], axis=1)
    _, _, cols, channels = rim.shape
    part = channels // 32
    core = lax.axis_index("core")
    source = lax.broadcasted_iota(jnp.int32, (channels, channels // 2), 0)
    target = lax.broadcasted_iota(jnp.int32, (channels, channels // 2), 1)
    wide = jnp.pad(rim, ((0, 0), (0, 0), (1, 1), (0, 0)))
    own, other = [], []
    for s in range(3):
        moved = wide[:, :, 2 - s : 2 - s + cols, :].reshape(-1, channels)
        for which, parts in ((core, own), (1 - core, other)):
            take = (source == (target // part) * 2 * part + which * part + target % part).astype(BF16)
            parts.append(
                lax.dot_general(take, moved, (((0,), (1,)), ((), ())), preferred_element_type=F32).astype(BF16)
            )
    return own + [swap_core(p) for p in other]


def sum_over_devices(partial):
    ny, nx, nzl, nzh = (lax.axis_size(a) for a in ("y", "x", "zl", "zh"))
    outs, width = partial.shape[1:]
    rows = outs // ny
    part = lax.all_to_all(partial.reshape(nx * ny, rows, width), ("x", "y"), 0, 0, tiled=True)
    part = jnp.sum(part.astype(F32), axis=0)
    part = part.reshape(nzl, rows // nzl, nzh, width // nzh).transpose(2, 0, 1, 3)
    part = part.reshape(nzh * nzl, rows // nzl, width // nzh)
    return jnp.sum(lax.all_to_all(part, ("zh", "zl"), 0, 0, tiled=True), axis=0)


def on_device(
    latents, conv_weight, conv_bias, query_weight, key_weight, value_weight, out_weight, cotangent
):
    above, below = edge_rows(latents)
    cot_above, cot_below = edge_rows(cotangent)
    count = math.prod(lax.axis_size(a) for a in FRAME)
    hidden = conv_silu(above, latents, below, conv_weight, conv_bias, count)
    blocked = lax.all_to_all(hidden, FRAME, 0, 0, tiled=True)
    cots = shifted_cotangent(cotangent, cot_above, cot_below)
    wqkv = jnp.concatenate([query_weight, key_weight, value_weight], axis=1)
    blocked, wqkv, *cots = lax.optimization_barrier((blocked, wqkv, *cots))
    pixel_mixed = attend(blocked.reshape(-1, *blocked.shape[2:]), wqkv, out_weight)
    sent = pixel_mixed.reshape(count, -1, *pixel_mixed.shape[1:])
    back = lax.all_to_all(sent, FRAME, 0, 0, tiled=True)
    mixed_frames = back.transpose(1, 2, 0, 3, 4).reshape(latents.shape)
    partial = kernel_grad(cots, (back, swap_core(back)), lax.axis_size("x"))
    return (mixed_frames, sum_over_devices(partial))


def solution(mesh):
    frame, tile = mesh.shape["frame"], mesh.shape["tile"]
    split = Mesh(
        mesh.devices.reshape(2, frame // 2, 4, tile // 8, 2), ("zh", "x", "y", "zl", "core")
    )
    in_specs = (
        P(FRAME, TILE, None, None),
        P(),
        P(),
        P(),
        P(),
        P(),
        P(),
        P(FRAME, TILE, None, None),
    )
    out_specs = (P(FRAME, TILE, None, None), P(TILE, FRAME))

    return jax.shard_map(
        on_device, mesh=split, in_specs=in_specs, out_specs=out_specs, check_vma=False
    )
```

time: 329 us -> 176 us (0.53)
  waiting for transfers between devices: 141 us -> 23.8 us
  Pallas kernels: 0 us -> 29.1 us
  matrix products: 30.3 us -> 6.45 us
  local copies, waits for them, and re-layouts: 30 us -> 7.71 us
  starting transfers between devices: 16.7 us -> 34.1 us
  blocking collectives: 89 us -> 71.7 us
  between operations: 14.4 us -> 0.88 us
  other arithmetic: 7.79 us -> 2.24 us
    reduce_scatter x2 -> x0, waiting for transfers between devices: 133 us -> none  [the longest x1 114 us: sum_by_chip(): return lax.psum_scatter(parts, chips, scatter_dimension=0, tiled=True)[0]]
    pallas_call x0 -> x3, Pallas kernels: none -> 29.1 us  [the longest x1 10.5 us: kernel_grad(): pl.pallas_call(grad_kernel, grid=(3,), in_specs=[cot_spec] * 6 + [mix_spe...]
    all_to_all x0 -> x2, waiting for transfers between devices: none -> 18.6 us  [the longest x1 11.3 us: sum_over_devices(): return jnp.sum(lax.all_to_all(part, ('zh', 'zl'), 0, 0, tiled=True), axis=0)]
    dot_general x7 -> x6, matrix products: 24.6 us -> 6.45 us  [shifted_cotangent(): lax.dot_general(take, moved, (((0,), (1,)), ((), ())), preferred_element_...]
    all_to_all x3 -> x2, blocking collectives: 89 us -> 71.7 us  [the longest x1 39.9 us: sum_over_devices(): lax.all_to_all(partial.reshape(nx * ny, rows, width), ('x', 'y'), 0, 0, t...]
    all_to_all x0 -> x2, starting transfers between devices: none -> 16.8 us  [the longest x1 10.9 us: on_device(): blocked = lax.all_to_all(hidden, FRAME, 0, 0, tiled=True)]
    reshape x4 -> x1, local copies, waits for them, and re-layouts: 11.5 us -> 0.25 us  [sum_over_devices(): part.reshape(nzl, rows // nzl, nzh, width // nzh).transpose(2, 0, 1, 3)]
    conv_general_dilated x1 -> x0, matrix products: 5.76 us -> none  [on_device(): lax.conv_general_dilated(padded, conv_weight, (1, 1), ((0, 0), (1, 1)), d...]
  transfers between devices with their start and end apart: 6 -> 10, of which waited for: 6 -> 5; matrix products, arithmetic and copies ran while one was open for 0% -> 6% of each run, Pallas kernels for 0% -> 6%
where the time goes in v1:
time: 176 us
  blocking collectives  71.7 us (41%)
  starting transfers between devices  34.1 us (19%)
  Pallas kernels  29.1 us (17%)
  waiting for transfers between devices  23.8 us (14%)
  local copies, waits for them, and re-layouts  7.71 us (4%)
  matrix products  6.45 us (4%)
  other arithmetic  2.24 us (1%)
    all_to_all x1, blocking collectives, sum_over_devices(): lax.all_to_all(partial.reshape(nx * ny, rows, width), ('x', 'y'), 0, 0, t...  39.9 us
    all_to_all x1, blocking collectives, on_device(): back = lax.all_to_all(sent, FRAME, 0, 0, tiled=True)  31.8 us
    ppermute x2, starting transfers between devices, edge_rows(): below = lax.ppermute(head, TILE, [(i + 1, i) for i in range(count - 1)])  12.7 us
    all_to_all x1, waiting for transfers between devices, sum_over_devices(): return jnp.sum(lax.all_to_all(part, ('zh', 'zl'), 0, 0, tiled=True), axis=0)  11.3 us
    all_to_all x1, starting transfers between devices, on_device(): blocked = lax.all_to_all(hidden, FRAME, 0, 0, tiled=True)  10.9 us
    pallas_call x1, Pallas kernels, kernel_grad(): pl.pallas_call(grad_kernel, grid=(3,), in_specs=[cot_spec] * 6 + [mix_spe...  10.5 us
    pallas_call x1, Pallas kernels, conv_silu(): pl.pallas_call(conv_kernel, grid=(3,), in_specs=[edge, pl.BlockSpec(own.s...  9.95 us
    pallas_call x1, Pallas kernels, attend(): pl.pallas_call(attention_kernel, grid=(rows,), in_specs=[spec, pl.BlockSp...  8.66 us
  transfers between devices with their start and end apart: 10, of which 5 were waited for; matrix products, arithmetic and copies ran while one was open for 6% of the time, Pallas kernels for 6%

profile of v1, /device:TPU:8, one launch (start us, length us, event | category | flops | bytes accessed | tf_op | source)
XLA Modules:
  0.0 175.9 jit_solution(17012564949956023799)
XLA Ops:
  0.7 1.2 fusion.18
  1.8 1.9 %collective-permute-start.2 = (bf16[2,1,128,512]{3,2,1,0:T(8,128)(2,1)S(1)}, bf16[2,1,128,512]{3,2,1,0:T(8,128)(2,1)S(1)}, u32[]{:S(2)}, u32[]{:S(2)}) collective-permute-start(bf16[2,1,128,512]{3,2,1,0:T(8,128)(2,1)S(1)} %get-tuple-element.21), channel_id=1, source_target_pairs={{0,1},{1,2},{2,3},{3,4},{4,5},{5,6},{6,7},{7,8},{8,9},{9,10},{10,1... | collective-permute-start | bytes 786440 | tf_op jit(solution)/shard_map/ppermute | solution.py:23
  3.8 6.3 %collective-permute-start.3 = (bf16[2,1,128,512]{3,2,1,0:T(8,128)(2,1)S(1)}, bf16[2,1,128,512]{3,2,1,0:T(8,128)(2,1)S(1)}, u32[]{:S(2)}, u32[]{:S(2)}) collective-permute-start(bf16[2,1,128,512]{3,2,1,0:T(8,128)(2,1)S(1)} %get-tuple-element.20), channel_id=1, source_target_pairs={{1,0},{2,1},{3,2},{4,3},{5,4},{6,5},{7,6},{8,7},{9,8},{10,9},{11,1... | collective-permute-start | bytes 786440 | tf_op jit(solution)/shard_map/ppermute | solution.py:24
  10.1 1.1 fusion.19
  11.2 1.9 %collective-permute-start = (bf16[2,1,128,512]{3,2,1,0:T(8,128)(2,1)S(1)}, bf16[2,1,128,512]{3,2,1,0:T(8,128)(2,1)S(1)}, u32[]{:S(2)}, u32[]{:S(2)}) collective-permute-start(bf16[2,1,128,512]{3,2,1,0:T(8,128)(2,1)S(1)} %get-tuple-element.23), channel_id=1, source_target_pairs={{0,1},{1,2},{2,3},{3,4},{4,5},{5,6},{6,7},{7,8},{8,9},{9,10},{10,1... | collective-permute-start | bytes 786440 | tf_op jit(solution)/shard_map/ppermute | solution.py:23
  13.1 6.3 %collective-permute-start.1 = (bf16[2,1,128,512]{3,2,1,0:T(8,128)(2,1)S(1)}, bf16[2,1,128,512]{3,2,1,0:T(8,128)(2,1)}, u32[]{:S(2)}, u32[]{:S(2)}) collective-permute-start(bf16[2,1,128,512]{3,2,1,0:T(8,128)(2,1)S(1)} %get-tuple-element.22), channel_id=1, source_target_pairs={{1,0},{2,1},{3,2},{4,3},{5,4},{6,5},{7,6},{8,7},{9,8},{10,9},{11,1... | collective-permute-start | bytes 786440 | tf_op jit(solution)/shard_map/ppermute | solution.py:24
  19.5 1.3 pad_maximum_fusion.wqkv_ref
  20.8 2.3 %collective-permute-done.above_ref = bf16[2,1,128,512]{3,2,1,0:T(8,128)(2,1)S(1)} collective-permute-done((bf16[2,1,128,512]{3,2,1,0:T(8,128)(2,1)S(1)}, bf16[2,1,128,512]{3,2,1,0:T(8,128)(2,1)S(1)}, u32[]{:S(2)}, u32[]{:S(2)}) %collective-permute-start) | collective-permute-done | bytes 262176 | tf_op jit(solution)/shard_map/ppermute | solution.py:23
  23.9 9.9 %conv_silu.1 = bf16[8,2,4,16,512]{4,3,2,1,0:T(8,128)(2,1)} custom-call(bf16[2,1,128,512]{3,2,1,0:T(8,128)(2,1)} %copy-done.10, bf16[2,4,128,512]{3,2,1,0:T(8,128)(2,1)} %own_ref.1, bf16[2,1,128,512]{3,2,1,0:T(8,128)(2,1)} %collective-permute-done.1.below_ref, bf16[3,3,512,512]{3,2,1,0:T(8,128)(2,1)} %weight_ref.1, f32[1,512]{1,0:T(1,128)} %bitcast.29), custom_call_target="tpu_custom_call" | custom-call | flops 5000000000 | bytes 8000000 | tf_op jit(solution)/shard_map/conv_silu/pallas_call | solution.py:74
  33.8 10.9 %all-to-all-start = ((bf16[8,2,4,16,512]{4,3,2,1,0:T(8,128)(2,1)}), bf16[8,2,4,16,512]{4,3,2,1,0:T(8,128)(2,1)S(1)}, u32[]{:S(2)}, u32[]{:S(2)}) async-start(bf16[8,2,4,16,512]{4,3,2,1,0:T(8,128)(2,1)} %conv_silu.1), calls=%async_computation | async-start | bytes 2097152 | tf_op jit(solution)/shard_map/all_to_all | solution.py:240
  48.4 1.5 convolution_convert_fusion.3.refs_2_
  49.9 1.5 convolution_convert_fusion.5.refs_0_
  51.4 1.5 convolution_convert_fusion.4.refs_1_
  53.0 7.3 %all-to-all-done = bf16[8,2,4,16,512]{4,3,2,1,0:T(8,128)(2,1)S(1)} async-done(((bf16[8,2,4,16,512]{4,3,2,1,0:T(8,128)(2,1)}), bf16[8,2,4,16,512]{4,3,2,1,0:T(8,128)(2,1)S(1)}, u32[]{:S(2)}, u32[]{:S(2)}) %all-to-all-start) | async-done | bytes 1048608 | tf_op jit(solution)/shard_map/all_to_all | solution.py:240
  60.3 1.0 copy-done.3
  61.3 8.7 %attend.1 = bf16[16,4,16,512]{3,2,1,0:T(8,128)(2,1)} custom-call(bf16[16,4,16,512]{3,2,1,0:T(8,128)(2,1)} %bitcast.26, bf16[512,1536]{1,0:T(8,128)(2,1)} %pad_maximum_fusion.wqkv_ref, bf16[512,512]{1,0:T(8,128)(2,1)} %wo_ref.1), custom_call_target="tpu_custom_call" | custom-call | flops 5000000000 | bytes 4000000 | tf_op jit(solution)/shard_map/attend/pallas_call | solution.py:135
  69.9 31.8 %all_to_all.20.refs_6_ = bf16[8,2,4,16,512]{4,3,2,1,0:T(8,128)(2,1)S(1)} all-to-all(bf16[8,2,4,16,512]{4,3,2,1,0:T(8,128)(2,1)} %bitcast.28), channel_id=1, replica_groups=mesh['zh'=2,'x'=4,'y'=4,'zl'=4,'core'=2] {'zh','x'}, dimensions={0} | all-to-all | bytes 2097152 | tf_op jit(solution)/shard_map/all_to_all | solution.py:246
  101.7 2.7 %collective-permute-done.7.refs_7_ = bf16[8,2,4,16,512]{4,3,2,1,0:T(8,128)(2,1)S(1)} collective-permute-done((bf16[8,2,4,16,512]{4,3,2,1,0:T(8,128)(2,1)S(1)}, bf16[8,2,4,16,512]{4,3,2,1,0:T(8,128)(2,1)S(1)}, u32[]{:S(2)}, u32[]{:S(2)}) %collective-permute-start.7) | collective-permute-done | bytes 1048608 | tf_op jit(solution)/shard_map/ppermute | solution.py:200
  104.4 1.0 copy-done.7
  105.4 10.5 %kernel_grad.1 = bf16[4,256,1152]{2,1,0:T(8,128)(2,1)} custom-call(bf16[256,1536]{1,0:T(8,128)(2,1)} %convolution_convert_fusion.5.refs_0_, bf16[256,1536]{1,0:T(8,128)(2,1)} %convolution_convert_fusion.4.refs_1_, bf16[256,1536]{1,0:T(8,128)(2,1)} %convolution_convert_fusion.3.refs_2_, bf16[256,1536]{1,0:T(8,128)(2,1)} %copy-done.8, ...), custom_call_target="tpu_custom_call" | custom-call | flops 5000000000 | bytes 8000000 | tf_op jit(solution)/shard_map/kernel_grad/pallas_call | solution.py:188
  115.8 39.9 %all_to_all.21 = bf16[16,64,1152]{2,1,0:T(8,128)(2,1)S(1)} all-to-all(bf16[16,64,1152]{2,1,0:T(8,128)(2,1)} %bitcast.18), channel_id=1, replica_groups=mesh['zh'=2,'x'=4,'y'=4,'zl'=4,'core'=2] {'x','y'}, dimensions={0} | all-to-all | bytes 4718592 | tf_op jit(solution)/shard_map/all_to_all | solution.py:226
  157.0 5.8 %all-to-all-start.3 = ((f32[8,16,576]{2,1,0:T(8,128)}), f32[8,16,576]{2,1,0:T(8,128)S(1)}, u32[]{:S(2)}, u32[]{:S(2)}) async-start(f32[8,16,576]{2,1,0:T(8,128)} %bitcast.10), calls=%async_computation.3 | async-start | bytes 655360 | tf_op jit(solution)/shard_map/all_to_all | solution.py:230
  162.9 1.1 copy.11
  163.9 11.3 %all-to-all-done.3 = f32[8,16,576]{2,1,0:T(8,128)S(1)} async-done(((f32[8,16,576]{2,1,0:T(8,128)}), f32[8,16,576]{2,1,0:T(8,128)S(1)}, u32[]{:S(2)}, u32[]{:S(2)}) %all-to-all-start.3) | async-done | bytes 294944 | tf_op jit(solution)/shard_map/all_to_all | solution.py:230
  (44 shorter events, 6.3 us)
Async XLA Ops:
  0.6 18.9 %copy-start.6 = (bf16[512,512]{1,0:T(8,128)(2,1)S(1)}, bf16[512,512]{1,0:T(8,128)(2,1)}, u32[]{:S(2)}) copy-start(bf16[512,512]{1,0:T(8,128)(2,1)} %param.11) | copy-start | bytes 1572868
  0.6 18.9 %copy-start.5 = (bf16[512,512]{1,0:T(8,128)(2,1)S(1)}, bf16[512,512]{1,0:T(8,128)(2,1)}, u32[]{:S(2)}) copy-start(bf16[512,512]{1,0:T(8,128)(2,1)} %param.12) | copy-start | bytes 1572868
  0.7 18.9 %copy-start.4 = (bf16[512,512]{1,0:T(8,128)(2,1)S(1)}, bf16[512,512]{1,0:T(8,128)(2,1)}, u32[]{:S(2)}) copy-start(bf16[512,512]{1,0:T(8,128)(2,1)} %param.13) | copy-start | bytes 1572868
  1.8 42.9 %collective-permute-start.2 = (bf16[2,1,128,512]{3,2,1,0:T(8,128)(2,1)S(1)}, bf16[2,1,128,512]{3,2,1,0:T(8,128)(2,1)S(1)}, u32[]{:S(2)}, u32[]{:S(2)}) collective-permute-start(bf16[2,1,128,512]{3,2,1,0:T(8,128)(2,1)S(1)} %get-tuple-element.21), channel_id=1, source_target_pairs={{0,1},{1,2},{2,3},{3,4},{4,5},{5,6},{6,7},{7,8},{8,9},{9,10},{10,1... | collective-permute-start | bytes 786440 | tf_op jit(solution)/shard_map/ppermute | solution.py:23
  3.8 41.1 %collective-permute-start.3 = (bf16[2,1,128,512]{3,2,1,0:T(8,128)(2,1)S(1)}, bf16[2,1,128,512]{3,2,1,0:T(8,128)(2,1)S(1)}, u32[]{:S(2)}, u32[]{:S(2)}) collective-permute-start(bf16[2,1,128,512]{3,2,1,0:T(8,128)(2,1)S(1)} %get-tuple-element.20), channel_id=1, source_target_pairs={{1,0},{2,1},{3,2},{4,3},{5,4},{6,5},{7,6},{8,7},{9,8},{10,9},{11,1... | collective-permute-start | bytes 786440 | tf_op jit(solution)/shard_map/ppermute | solution.py:24
  11.2 12.0 %collective-permute-start = (bf16[2,1,128,512]{3,2,1,0:T(8,128)(2,1)S(1)}, bf16[2,1,128,512]{3,2,1,0:T(8,128)(2,1)S(1)}, u32[]{:S(2)}, u32[]{:S(2)}) collective-permute-start(bf16[2,1,128,512]{3,2,1,0:T(8,128)(2,1)S(1)} %get-tuple-element.23), channel_id=1, source_target_pairs={{0,1},{1,2},{2,3},{3,4},{4,5},{5,6},{6,7},{7,8},{8,9},{9,10},{10,1... | collective-permute-start | bytes 786440 | tf_op jit(solution)/shard_map/ppermute | solution.py:23
  13.1 10.2 %collective-permute-start.1 = (bf16[2,1,128,512]{3,2,1,0:T(8,128)(2,1)S(1)}, bf16[2,1,128,512]{3,2,1,0:T(8,128)(2,1)}, u32[]{:S(2)}, u32[]{:S(2)}) collective-permute-start(bf16[2,1,128,512]{3,2,1,0:T(8,128)(2,1)S(1)} %get-tuple-element.22), channel_id=1, source_target_pairs={{1,0},{2,1},{3,2},{4,3},{5,4},{6,5},{7,6},{8,7},{9,8},{10,9},{11,1... | collective-permute-start | bytes 786440 | tf_op jit(solution)/shard_map/ppermute | solution.py:24
  23.2 0.7 copy-start.10
  33.8 11.0 %copy-start.2 = (bf16[2,4,128,512]{3,2,1,0:T(8,128)(2,1)S(1)}, bf16[2,4,128,512]{3,2,1,0:T(8,128)(2,1)}, u32[]{:S(2)}) copy-start(bf16[2,4,128,512]{3,2,1,0:T(8,128)(2,1)} %param.15) | copy-start | bytes 3145732
  33.8 26.5 %all-to-all-start = ((bf16[8,2,4,16,512]{4,3,2,1,0:T(8,128)(2,1)}), bf16[8,2,4,16,512]{4,3,2,1,0:T(8,128)(2,1)S(1)}, u32[]{:S(2)}, u32[]{:S(2)}) async-start(bf16[8,2,4,16,512]{4,3,2,1,0:T(8,128)(2,1)} %conv_silu.1), calls=%async_computation | async-start | bytes 2097152 | tf_op jit(solution)/shard_map/all_to_all | solution.py:240
  46.3 6.6 %collective-permute-start.4 = (bf16[256,1536]{1,0:T(8,128)(2,1)S(1)}, bf16[256,1536]{1,0:T(8,128)(2,1)S(1)}, u32[]{:S(2)}, u32[]{:S(2)}) collective-permute-start(bf16[256,1536]{1,0:T(8,128)(2,1)S(1)} %convolution_convert_fusion.2), channel_id=1, source_target_pairs={{0,1},{1,0},{2,3},{3,2},{4,5},{5,4},{6,7},{7,6},{8,9},{9,8},{10,11... | collective-permute-start | bytes 2359304 | tf_op jit(solution)/shard_map/ppermute | solution.py:200
  47.1 5.9 %collective-permute-start.6 = (bf16[256,1536]{1,0:T(8,128)(2,1)S(1)}, bf16[256,1536]{1,0:T(8,128)(2,1)S(1)}, u32[]{:S(2)}, u32[]{:S(2)}) collective-permute-start(bf16[256,1536]{1,0:T(8,128)(2,1)S(1)} %convolution_convert_fusion), channel_id=1, source_target_pairs={{0,1},{1,0},{2,3},{3,2},{4,5},{5,4},{6,7},{7,6},{8,9},{9,8},{10,11... | collective-permute-start | bytes 2359304 | tf_op jit(solution)/shard_map/ppermute | solution.py:200
  48.3 4.7 %collective-permute-start.5 = (bf16[256,1536]{1,0:T(8,128)(2,1)S(1)}, bf16[256,1536]{1,0:T(8,128)(2,1)}, u32[]{:S(2)}, u32[]{:S(2)}) collective-permute-start(bf16[256,1536]{1,0:T(8,128)(2,1)S(1)} %convolution_convert_fusion.1), channel_id=1, source_target_pairs={{0,1},{1,0},{2,3},{3,2},{4,5},{5,4},{6,7},{7,6},{8,9},{9,8},{10,11... | collective-permute-start | bytes 2359304 | tf_op jit(solution)/shard_map/ppermute | solution.py:200
  53.0 17.0 %copy-start.8 = (bf16[256,1536]{1,0:T(8,128)(2,1)}, bf16[256,1536]{1,0:T(8,128)(2,1)S(1)}, u32[]{:S(2)}) copy-start(bf16[256,1536]{1,0:T(8,128)(2,1)S(1)} %collective-permute-done.4.refs_3_) | copy-start | bytes 2359300
  53.0 17.0 %copy-start.9 = (bf16[256,1536]{1,0:T(8,128)(2,1)}, bf16[256,1536]{1,0:T(8,128)(2,1)S(1)}, u32[]{:S(2)}) copy-start(bf16[256,1536]{1,0:T(8,128)(2,1)S(1)} %collective-permute-done.6.refs_5_) | copy-start | bytes 2359300
  60.3 1.0 copy-start.3
  101.7 2.7 %copy-start = (bf16[8,2,4,16,512]{4,3,2,1,0:T(8,128)(2,1)}, bf16[8,2,4,16,512]{4,3,2,1,0:T(8,128)(2,1)S(1)}, u32[]{:S(2)}) copy-start(bf16[8,2,4,16,512]{4,3,2,1,0:T(8,128)(2,1)S(1)} %all_to_all.20.refs_6_) | copy-start | bytes 3145732
  101.7 2.7 %collective-permute-start.7 = (bf16[8,2,4,16,512]{4,3,2,1,0:T(8,128)(2,1)S(1)}, bf16[8,2,4,16,512]{4,3,2,1,0:T(8,128)(2,1)S(1)}, u32[]{:S(2)}, u32[]{:S(2)}) collective-permute-start(bf16[8,2,4,16,512]{4,3,2,1,0:T(8,128)(2,1)S(1)} %all_to_all.20.refs_6_), channel_id=1, source_target_pairs={{0,1},{1,0},{2,3},{3,2},{4,5},{5,4},{6,7},{7,6},{8,9},{9,8},{10,11... | collective-permute-start | bytes 3145736 | tf_op jit(solution)/shard_map/ppermute | solution.py:200
  104.4 1.0 copy-start.7
  156.0 6.9 %copy-start.1 = (bf16[8,2,4,16,512]{4,3,2,1,0:T(8,128)(2,1)S(1)}, bf16[8,2,4,16,512]{4,3,2,1,0:T(8,128)(2,1)}, u32[]{:S(2)}) copy-start(bf16[8,2,4,16,512]{4,3,2,1,0:T(8,128)(2,1)} %copy-done) | copy-start | bytes 3145732
  157.0 18.2 %all-to-all-start.3 = ((f32[8,16,576]{2,1,0:T(8,128)}), f32[8,16,576]{2,1,0:T(8,128)S(1)}, u32[]{:S(2)}, u32[]{:S(2)}) async-start(f32[8,16,576]{2,1,0:T(8,128)} %bitcast.10), calls=%async_computation.3 | async-start | bytes 655360 | tf_op jit(solution)/shard_map/all_to_all | solution.py:230

commit v2 on v1

--- a/solution.py
+++ b/solution.py
@@ -40,14 +40,12 @@
     column = lax.broadcasted_iota(jnp.int32, (pixels, 1), 0) % cols
     blocks = out_ref.shape[0]
     for f in range(frames):
-        part = None
-        for r in range(3):
-            term = jnp.dot(
-                rows_ref[f, r * cols : r * cols + pixels],
-                weight_ref[r, 0],
-                preferred_element_type=F32,
-            )
-            part = term if part is None else part + term
+        taps = [rows_ref[f, r * cols : r * cols + pixels] for r in range(3)]
+        part = jnp.dot(
+            jnp.concatenate(taps, axis=1),
+            weight_ref[...].reshape(3 * channels, channels),
+            preferred_element_type=F32,
+        )
 
         @pl.when(s == 0)
         def _():
@@ -149,48 +147,46 @@
 
 def grad_kernel(*refs):
     cots, mixes, out_ref = (refs[:3], refs[3:6]), refs[6:8], refs[8]
-    r = pl.program_id(0)
     blocks, frames, height, width, channels = mixes[0].shape
     cols = blocks * width
     pixels = height * cols
     outs = cots[0][0].shape[0]
-    acc = None
-    for side in range(2):
-        for f in range(frames):
-            mix = jnp.concatenate(
-                [mixes[side][b, f, y] for y in range(height) for b in range(blocks)], axis=0
-            )
-            start = pl.multiple_of(f * (pixels + 2 * cols) + (2 - r) * cols, cols)
-            cot = jnp.concatenate([c[:, pl.ds(start, pixels)] for c in cots[side]], axis=0)
-            part = jnp.dot(cot, mix, preferred_element_type=F32)
-            acc = part if acc is None else acc + part
-    flat = jnp.concatenate([acc[s * outs : (s + 1) * outs] for s in range(3)], axis=1).astype(BF16)
+    sides = [(side, f) for side in range(2) for f in range(frames)]
+    mix = jnp.concatenate(
+        [mixes[w][b, f, y] for w, f in sides for y in range(height) for b in range(blocks)], axis=0
+    )
     places = out_ref.shape[0]
     block = channels * 9 // (2 * places)
-    for step in range(3):
-
-        @pl.when(r == step)
-        def _():
-            lo = step * 3 * channels
-            for k in range(2 * places):
-                a, b = max(lo, k * block), min(lo + 3 * channels, (k + 1) * block)
-                if a < b:
-                    to = (k // places) * block + a - k * block
-                    out_ref[k % places, :, to : to + b - a] = flat[:, a - lo : b - lo]
+    for r in range(3):
+        lines = []
+        for s in range(3):
+            pieces = []
+            for w, f in sides:
+                start = f * (pixels + 2 * cols) + (2 - r) * cols
+                pieces.append(cots[w][s][:, start : start + pixels])
+            lines.append(jnp.concatenate(pieces, axis=1))
+        acc = jnp.dot(jnp.concatenate(lines, axis=0), mix, preferred_element_type=F32)
+        flat = [acc[s * outs : (s + 1) * outs] for s in range(3)]
+        flat = jnp.concatenate(flat, axis=1).astype(BF16)
+        lo = r * 3 * channels
+        for k in range(2 * places):
+            a, b = max(lo, k * block), min(lo + 3 * channels, (k + 1) * block)
+            if a < b:
+                to = (k // places) * block + a - k * block
+                out_ref[k % places, :, to : to + b - a] = flat[:, a - lo : b - lo]
 
 
 def kernel_grad(cots, mixes, places):
-    outs, width = cots[0].shape
+    outs, _ = cots[0].shape
     channels = mixes[0].shape[-1]
     out_shape = (places, outs, 9 * channels // places)
-    cot_spec = pl.BlockSpec((outs, width), lambda r: (0, 0))
-    mix_spec = pl.BlockSpec(mixes[0].shape, lambda r: (0, 0, 0, 0, 0))
+    whole = pl.BlockSpec(memory_space=pltpu.VMEM)
     return pl.pallas_call(
         grad_kernel,
-        grid=(3,),
-        in_specs=[cot_spec] * 6 + [mix_spec] * 2,
-        out_specs=pl.BlockSpec(out_shape, lambda r: (0, 0, 0)),
+        in_specs=[whole] * 8,
+        out_specs=whole,
         out_shape=jax.ShapeDtypeStruct(out_shape, BF16),
+        compiler_params=pltpu.CompilerParams(vmem_limit_bytes=40 * 2**20),
         cost_estimate=pl.CostEstimate(flops=5 * 10**9, bytes_accessed=8 * 10**6, transcendentals=0),
         name="kernel_grad",
     )(*cots, *mixes)
@@ -224,10 +220,11 @@
     outs, width = partial.shape[1:]
     rows = outs // ny
     part = lax.all_to_all(partial.reshape(nx * ny, rows, width), ("x", "y"), 0, 0, tiled=True)
-    part = jnp.sum(part.astype(F32), axis=0)
+    part = lax.optimization_barrier(jnp.sum(part.astype(F32), axis=0))
     part = part.reshape(nzl, rows // nzl, nzh, width // nzh).transpose(2, 0, 1, 3)
-    part = part.reshape(nzh * nzl, rows // nzl, width // nzh)
-    return jnp.sum(lax.all_to_all(part, ("zh", "zl"), 0, 0, tiled=True), axis=0)
+    part = part.reshape(nzh * nzl, rows // nzl, width // nzh).astype(BF16)
+    part = lax.all_to_all(part, ("zh", "zl"), 0, 0, tiled=True)
+    return jnp.sum(part.astype(F32), axis=0)
 
 
 def on_device(

time: 176 us -> 166 us (0.943)
  Pallas kernels: 29.1 us -> 23.7 us
  waiting for transfers between devices: 23.8 us -> 21 us
  blocking collectives: 71.7 us -> 69.3 us
    pallas_call x1, Pallas kernels: 10.5 us -> 5.06 us  [kernel_grad(): pl.pallas_call(grad_kernel, in_specs=[whole] * 8, out_specs=whole, out_sh...]
    all_to_all x1, waiting for transfers between devices: 11.3 us -> 8.37 us  [sum_over_devices(): part = lax.all_to_all(part, ('zh', 'zl'), 0, 0, tiled=True)]
    all_to_all x1, blocking collectives: 39.9 us -> 37.5 us  [sum_over_devices(): lax.all_to_all(partial.reshape(nx * ny, rows, width), ('x', 'y'), 0, 0, t...]
  transfers between devices with their start and end apart: 10 -> 10, of which waited for: 5 -> 5; matrix products, arithmetic and copies ran while one was open for 6% -> 7% of each run, Pallas kernels for 6% -> 6%
where the time goes in v2:
time: 166 us; the launch traced here: 165 us
  blocking collectives  69.3 us (42%)
  starting transfers between devices  35.2 us (21%)
  Pallas kernels  23.7 us (14%)
  waiting for transfers between devices  21 us (13%)
  local copies, waits for them, and re-layouts  6.78 us (4%)
  matrix products  6.43 us (4%)
  other arithmetic  2.24 us (1%)
    all_to_all x1, blocking collectives, sum_over_devices(): lax.all_to_all(partial.reshape(nx * ny, rows, width), ('x', 'y'), 0, 0, t...  37.5 us
    all_to_all x1, blocking collectives, on_device(): back = lax.all_to_all(sent, FRAME, 0, 0, tiled=True)  31.8 us
    ppermute x2, starting transfers between devices, edge_rows(): below = lax.ppermute(head, TILE, [(i + 1, i) for i in range(count - 1)])  12.7 us
    all_to_all x1, starting transfers between devices, on_device(): blocked = lax.all_to_all(hidden, FRAME, 0, 0, tiled=True)  10.9 us
    pallas_call x1, Pallas kernels, conv_silu(): pl.pallas_call(conv_kernel, grid=(3,), in_specs=[edge, pl.BlockSpec(own.s...  9.95 us
    pallas_call x1, Pallas kernels, attend(): pl.pallas_call(attention_kernel, grid=(rows,), in_specs=[spec, pl.BlockSp...  8.65 us
    all_to_all x1, waiting for transfers between devices, sum_over_devices(): part = lax.all_to_all(part, ('zh', 'zl'), 0, 0, tiled=True)  8.37 us
    all_to_all x1, waiting for transfers between devices, on_device(): blocked = lax.all_to_all(hidden, FRAME, 0, 0, tiled=True)  7.4 us
  transfers between devices with their start and end apart: 10, of which 5 were waited for; matrix products, arithmetic and copies ran while one was open for 7% of the time, Pallas kernels for 6%

profile of v2, /device:TPU:8, one launch (start us, length us, event | category | flops | bytes accessed | tf_op | source)
XLA Modules:
  0.0 165.4 jit_solution(17628589603179895959)
XLA Ops:
  0.7 1.2 fusion.18
  1.8 1.9 %collective-permute-start.2 = (bf16[2,1,128,512]{3,2,1,0:T(8,128)(2,1)S(1)}, bf16[2,1,128,512]{3,2,1,0:T(8,128)(2,1)S(1)}, u32[]{:S(2)}, u32[]{:S(2)}) collective-permute-start(bf16[2,1,128,512]{3,2,1,0:T(8,128)(2,1)S(1)} %get-tuple-element.21), channel_id=1, source_target_pairs={{0,1},{1,2},{2,3},{3,4},{4,5},{5,6},{6,7},{7,8},{8,9},{9,10},{10,1... | collective-permute-start | bytes 786440 | tf_op jit(solution)/shard_map/ppermute | solution.py:23
  3.8 6.3 %collective-permute-start.3 = (bf16[2,1,128,512]{3,2,1,0:T(8,128)(2,1)S(1)}, bf16[2,1,128,512]{3,2,1,0:T(8,128)(2,1)S(1)}, u32[]{:S(2)}, u32[]{:S(2)}) collective-permute-start(bf16[2,1,128,512]{3,2,1,0:T(8,128)(2,1)S(1)} %get-tuple-element.20), channel_id=1, source_target_pairs={{1,0},{2,1},{3,2},{4,3},{5,4},{6,5},{7,6},{8,7},{9,8},{10,9},{11,1... | collective-permute-start | bytes 786440 | tf_op jit(solution)/shard_map/ppermute | solution.py:24
  10.1 1.1 fusion.19
  11.2 1.9 %collective-permute-start = (bf16[2,1,128,512]{3,2,1,0:T(8,128)(2,1)S(1)}, bf16[2,1,128,512]{3,2,1,0:T(8,128)(2,1)S(1)}, u32[]{:S(2)}, u32[]{:S(2)}) collective-permute-start(bf16[2,1,128,512]{3,2,1,0:T(8,128)(2,1)S(1)} %get-tuple-element.23), channel_id=1, source_target_pairs={{0,1},{1,2},{2,3},{3,4},{4,5},{5,6},{6,7},{7,8},{8,9},{9,10},{10,1... | collective-permute-start | bytes 786440 | tf_op jit(solution)/shard_map/ppermute | solution.py:23
  13.1 6.3 %collective-permute-start.1 = (bf16[2,1,128,512]{3,2,1,0:T(8,128)(2,1)S(1)}, bf16[2,1,128,512]{3,2,1,0:T(8,128)(2,1)}, u32[]{:S(2)}, u32[]{:S(2)}) collective-permute-start(bf16[2,1,128,512]{3,2,1,0:T(8,128)(2,1)S(1)} %get-tuple-element.22), channel_id=1, source_target_pairs={{1,0},{2,1},{3,2},{4,3},{5,4},{6,5},{7,6},{8,7},{9,8},{10,9},{11,1... | collective-permute-start | bytes 786440 | tf_op jit(solution)/shard_map/ppermute | solution.py:24
  19.5 1.3 pad_maximum_fusion.wqkv_ref
  20.8 2.3 %collective-permute-done.above_ref = bf16[2,1,128,512]{3,2,1,0:T(8,128)(2,1)S(1)} collective-permute-done((bf16[2,1,128,512]{3,2,1,0:T(8,128)(2,1)S(1)}, bf16[2,1,128,512]{3,2,1,0:T(8,128)(2,1)S(1)}, u32[]{:S(2)}, u32[]{:S(2)}) %collective-permute-start) | collective-permute-done | bytes 262176 | tf_op jit(solution)/shard_map/ppermute | solution.py:23
  23.9 9.9 %conv_silu.1 = bf16[8,2,4,16,512]{4,3,2,1,0:T(8,128)(2,1)} custom-call(bf16[2,1,128,512]{3,2,1,0:T(8,128)(2,1)} %copy-done.7, bf16[2,4,128,512]{3,2,1,0:T(8,128)(2,1)} %own_ref.1, bf16[2,1,128,512]{3,2,1,0:T(8,128)(2,1)} %collective-permute-done.1.below_ref, bf16[3,3,512,512]{3,2,1,0:T(8,128)(2,1)} %weight_ref.1, f32[1,512]{1,0:T(1,128)} %bitcast.28), custom_call_target="tpu_custom_call" | custom-call | flops 5000000000 | bytes 8000000 | tf_op jit(solution)/shard_map/conv_silu/pallas_call | solution.py:72
  33.8 10.9 %all-to-all-start = ((bf16[8,2,4,16,512]{4,3,2,1,0:T(8,128)(2,1)}), bf16[8,2,4,16,512]{4,3,2,1,0:T(8,128)(2,1)}, u32[]{:S(2)}, u32[]{:S(2)}) async-start(bf16[8,2,4,16,512]{4,3,2,1,0:T(8,128)(2,1)} %conv_silu.1), calls=%async_computation | async-start | bytes 2097152 | tf_op jit(solution)/shard_map/all_to_all | solution.py:237
  44.9 0.8 pad_slice_fusion
  48.4 1.5 convolution_convert_fusion.3.refs_2_
  49.9 1.5 convolution_convert_fusion.5.refs_0_
  51.4 1.5 convolution_convert_fusion.4.refs_1_
  53.0 7.4 %all-to-all-done = bf16[8,2,4,16,512]{4,3,2,1,0:T(8,128)(2,1)} async-done(((bf16[8,2,4,16,512]{4,3,2,1,0:T(8,128)(2,1)}), bf16[8,2,4,16,512]{4,3,2,1,0:T(8,128)(2,1)}, u32[]{:S(2)}, u32[]{:S(2)}) %all-to-all-start) | async-done | bytes 1048608 | tf_op jit(solution)/shard_map/all_to_all | solution.py:237
  60.4 8.7 %attend.1 = bf16[16,4,16,512]{3,2,1,0:T(8,128)(2,1)} custom-call(bf16[16,4,16,512]{3,2,1,0:T(8,128)(2,1)} %bitcast.4.x_ref, bf16[512,1536]{1,0:T(8,128)(2,1)} %pad_maximum_fusion.wqkv_ref, bf16[512,512]{1,0:T(8,128)(2,1)} %wo_ref.1), custom_call_target="tpu_custom_call" | custom-call | flops 5000000000 | bytes 4000000 | tf_op jit(solution)/shard_map/attend/pallas_call | solution.py:133
  69.0 31.8 %all_to_all.20.refs_6_ = bf16[8,2,4,16,512]{4,3,2,1,0:T(8,128)(2,1)S(1)} all-to-all(bf16[8,2,4,16,512]{4,3,2,1,0:T(8,128)(2,1)} %bitcast.26), channel_id=1, replica_groups=mesh['zh'=2,'x'=4,'y'=4,'zl'=4,'core'=2] {'zh','x'}, dimensions={0} | all-to-all | bytes 2097152 | tf_op jit(solution)/shard_map/all_to_all | solution.py:243
  100.8 2.7 %collective-permute-done.7.refs_7_ = bf16[8,2,4,16,512]{4,3,2,1,0:T(8,128)(2,1)S(1)} collective-permute-done((bf16[8,2,4,16,512]{4,3,2,1,0:T(8,128)(2,1)S(1)}, bf16[8,2,4,16,512]{4,3,2,1,0:T(8,128)(2,1)S(1)}, u32[]{:S(2)}, u32[]{:S(2)}) %collective-permute-start.7) | collective-permute-done | bytes 1048608 | tf_op jit(solution)/shard_map/ppermute | solution.py:196
  103.5 1.1 copy-done.2
  104.6 5.1 %kernel_grad.1 = bf16[4,256,1152]{2,1,0:T(8,128)(2,1)S(1)} custom-call(bf16[256,1536]{1,0:T(8,128)(2,1)S(1)} %copy-done.1, bf16[256,1536]{1,0:T(8,128)(2,1)S(1)} %copy-done.2, bf16[256,1536]{1,0:T(8,128)(2,1)S(1)} %copy-done, bf16[256,1536]{1,0:T(8,128)(2,1)S(1)} %collective-permute-done.4.refs_3_, bf16[256,1536]{1,0:T(8,128)(2,1)S(1)} %collective-permute-done.5.refs_4_, ...), custom_call_target="tpu_custom_call" | custom-call | flops 5000000000 | bytes 8000000 | tf_op jit(solution)/shard_map/kernel_grad/pallas_call | solution.py:184
  109.7 37.5 %all_to_all.21 = bf16[16,64,1152]{2,1,0:T(8,128)(2,1)S(1)} all-to-all(bf16[16,64,1152]{2,1,0:T(8,128)(2,1)S(1)} %bitcast.18), channel_id=1, replica_groups=mesh['zh'=2,'x'=4,'y'=4,'zl'=4,'core'=2] {'x','y'}, dimensions={0} | all-to-all | bytes 4718592 | tf_op jit(solution)/shard_map/all_to_all | solution.py:222
  148.3 7.0 %all-to-all-start.3 = ((bf16[8,16,576]{2,1,0:T(8,128)(2,1)}), bf16[8,16,576]{2,1,0:T(8,128)(2,1)S(1)}, u32[]{:S(2)}, u32[]{:S(2)}) async-start(bf16[8,16,576]{2,1,0:T(8,128)(2,1)} %bitcast.10), calls=%async_computation.3 | async-start | bytes 327680 | tf_op jit(solution)/shard_map/all_to_all | solution.py:226
  155.3 1.1 copy.11
  156.3 8.4 %all-to-all-done.3 = bf16[8,16,576]{2,1,0:T(8,128)(2,1)S(1)} async-done(((bf16[8,16,576]{2,1,0:T(8,128)(2,1)}), bf16[8,16,576]{2,1,0:T(8,128)(2,1)S(1)}, u32[]{:S(2)}, u32[]{:S(2)}) %all-to-all-start.3) | async-done | bytes 147488 | tf_op jit(solution)/shard_map/all_to_all | solution.py:226
  (38 shorter events, 5.4 us)
Async XLA Ops:
  0.6 18.9 %copy-start.6 = (bf16[512,512]{1,0:T(8,128)(2,1)S(1)}, bf16[512,512]{1,0:T(8,128)(2,1)}, u32[]{:S(2)}) copy-start(bf16[512,512]{1,0:T(8,128)(2,1)} %param.11) | copy-start | bytes 1572868
  0.6 18.9 %copy-start.5 = (bf16[512,512]{1,0:T(8,128)(2,1)S(1)}, bf16[512,512]{1,0:T(8,128)(2,1)}, u32[]{:S(2)}) copy-start(bf16[512,512]{1,0:T(8,128)(2,1)} %param.12) | copy-start | bytes 1572868
  0.7 18.9 %copy-start.4 = (bf16[512,512]{1,0:T(8,128)(2,1)S(1)}, bf16[512,512]{1,0:T(8,128)(2,1)}, u32[]{:S(2)}) copy-start(bf16[512,512]{1,0:T(8,128)(2,1)} %param.13) | copy-start | bytes 1572868
  1.8 42.9 %collective-permute-start.2 = (bf16[2,1,128,512]{3,2,1,0:T(8,128)(2,1)S(1)}, bf16[2,1,128,512]{3,2,1,0:T(8,128)(2,1)S(1)}, u32[]{:S(2)}, u32[]{:S(2)}) collective-permute-start(bf16[2,1,128,512]{3,2,1,0:T(8,128)(2,1)S(1)} %get-tuple-element.21), channel_id=1, source_target_pairs={{0,1},{1,2},{2,3},{3,4},{4,5},{5,6},{6,7},{7,8},{8,9},{9,10},{10,1... | collective-permute-start | bytes 786440 | tf_op jit(solution)/shard_map/ppermute | solution.py:23
  3.8 41.1 %collective-permute-start.3 = (bf16[2,1,128,512]{3,2,1,0:T(8,128)(2,1)S(1)}, bf16[2,1,128,512]{3,2,1,0:T(8,128)(2,1)S(1)}, u32[]{:S(2)}, u32[]{:S(2)}) collective-permute-start(bf16[2,1,128,512]{3,2,1,0:T(8,128)(2,1)S(1)} %get-tuple-element.20), channel_id=1, source_target_pairs={{1,0},{2,1},{3,2},{4,3},{5,4},{6,5},{7,6},{8,7},{9,8},{10,9},{11,1... | collective-permute-start | bytes 786440 | tf_op jit(solution)/shard_map/ppermute | solution.py:24
  11.2 12.0 %collective-permute-start = (bf16[2,1,128,512]{3,2,1,0:T(8,128)(2,1)S(1)}, bf16[2,1,128,512]{3,2,1,0:T(8,128)(2,1)S(1)}, u32[]{:S(2)}, u32[]{:S(2)}) collective-permute-start(bf16[2,1,128,512]{3,2,1,0:T(8,128)(2,1)S(1)} %get-tuple-element.23), channel_id=1, source_target_pairs={{0,1},{1,2},{2,3},{3,4},{4,5},{5,6},{6,7},{7,8},{8,9},{9,10},{10,1... | collective-permute-start | bytes 786440 | tf_op jit(solution)/shard_map/ppermute | solution.py:23
  13.1 10.2 %collective-permute-start.1 = (bf16[2,1,128,512]{3,2,1,0:T(8,128)(2,1)S(1)}, bf16[2,1,128,512]{3,2,1,0:T(8,128)(2,1)}, u32[]{:S(2)}, u32[]{:S(2)}) collective-permute-start(bf16[2,1,128,512]{3,2,1,0:T(8,128)(2,1)S(1)} %get-tuple-element.22), channel_id=1, source_target_pairs={{1,0},{2,1},{3,2},{4,3},{5,4},{6,5},{7,6},{8,7},{9,8},{10,9},{11,1... | collective-permute-start | bytes 786440 | tf_op jit(solution)/shard_map/ppermute | solution.py:24
  23.2 0.7 copy-start.7
  33.8 11.0 %copy-start.3 = (bf16[2,4,128,512]{3,2,1,0:T(8,128)(2,1)S(1)}, bf16[2,4,128,512]{3,2,1,0:T(8,128)(2,1)}, u32[]{:S(2)}) copy-start(bf16[2,4,128,512]{3,2,1,0:T(8,128)(2,1)} %param.15) | copy-start | bytes 3145732
  33.8 26.5 %all-to-all-start = ((bf16[8,2,4,16,512]{4,3,2,1,0:T(8,128)(2,1)}), bf16[8,2,4,16,512]{4,3,2,1,0:T(8,128)(2,1)}, u32[]{:S(2)}, u32[]{:S(2)}) async-start(bf16[8,2,4,16,512]{4,3,2,1,0:T(8,128)(2,1)} %conv_silu.1), calls=%async_computation | async-start | bytes 2097152 | tf_op jit(solution)/shard_map/all_to_all | solution.py:237
  46.3 6.6 %collective-permute-start.4 = (bf16[256,1536]{1,0:T(8,128)(2,1)S(1)}, bf16[256,1536]{1,0:T(8,128)(2,1)S(1)}, u32[]{:S(2)}, u32[]{:S(2)}) collective-permute-start(bf16[256,1536]{1,0:T(8,128)(2,1)S(1)} %convolution_convert_fusion.2), channel_id=1, source_target_pairs={{0,1},{1,0},{2,3},{3,2},{4,5},{5,4},{6,7},{7,6},{8,9},{9,8},{10,11... | collective-permute-start | bytes 2359304 | tf_op jit(solution)/shard_map/ppermute | solution.py:196
  47.1 5.9 %collective-permute-start.6 = (bf16[256,1536]{1,0:T(8,128)(2,1)S(1)}, bf16[256,1536]{1,0:T(8,128)(2,1)S(1)}, u32[]{:S(2)}, u32[]{:S(2)}) collective-permute-start(bf16[256,1536]{1,0:T(8,128)(2,1)S(1)} %convolution_convert_fusion), channel_id=1, source_target_pairs={{0,1},{1,0},{2,3},{3,2},{4,5},{5,4},{6,7},{7,6},{8,9},{9,8},{10,11... | collective-permute-start | bytes 2359304 | tf_op jit(solution)/shard_map/ppermute | solution.py:196
  48.3 4.7 %collective-permute-start.5 = (bf16[256,1536]{1,0:T(8,128)(2,1)S(1)}, bf16[256,1536]{1,0:T(8,128)(2,1)S(1)}, u32[]{:S(2)}, u32[]{:S(2)}) collective-permute-start(bf16[256,1536]{1,0:T(8,128)(2,1)S(1)} %convolution_convert_fusion.1), channel_id=1, source_target_pairs={{0,1},{1,0},{2,3},{3,2},{4,5},{5,4},{6,7},{7,6},{8,9},{9,8},{10,11... | collective-permute-start | bytes 2359304 | tf_op jit(solution)/shard_map/ppermute | solution.py:196
  69.0 34.5 %copy-start = (bf16[256,1536]{1,0:T(8,128)(2,1)S(1)}, bf16[256,1536]{1,0:T(8,128)(2,1)}, u32[]{:S(2)}) copy-start(bf16[256,1536]{1,0:T(8,128)(2,1)} %convolution_convert_fusion.3.refs_2_) | copy-start | bytes 2359300
  69.0 34.5 %copy-start.1 = (bf16[256,1536]{1,0:T(8,128)(2,1)S(1)}, bf16[256,1536]{1,0:T(8,128)(2,1)}, u32[]{:S(2)}) copy-start(bf16[256,1536]{1,0:T(8,128)(2,1)} %convolution_convert_fusion.5.refs_0_) | copy-start | bytes 2359300
  100.8 2.7 %collective-permute-start.7 = (bf16[8,2,4,16,512]{4,3,2,1,0:T(8,128)(2,1)S(1)}, bf16[8,2,4,16,512]{4,3,2,1,0:T(8,128)(2,1)S(1)}, u32[]{:S(2)}, u32[]{:S(2)}) collective-permute-start(bf16[8,2,4,16,512]{4,3,2,1,0:T(8,128)(2,1)S(1)} %all_to_all.20.refs_6_), channel_id=1, source_target_pairs={{0,1},{1,0},{2,3},{3,2},{4,5},{5,4},{6,7},{7,6},{8,9},{9,8},{10,11... | collective-permute-start | bytes 3145736 | tf_op jit(solution)/shard_map/ppermute | solution.py:196
  103.5 1.1 copy-start.2
  148.3 16.4 %all-to-all-start.3 = ((bf16[8,16,576]{2,1,0:T(8,128)(2,1)}), bf16[8,16,576]{2,1,0:T(8,128)(2,1)S(1)}, u32[]{:S(2)}, u32[]{:S(2)}) async-start(bf16[8,16,576]{2,1,0:T(8,128)(2,1)} %bitcast.10), calls=%async_computation.3 | async-start | bytes 327680 | tf_op jit(solution)/shard_map/all_to_all | solution.py:226

commit v3 on v2

--- a/solution.py
+++ b/solution.py
@@ -67,17 +67,17 @@
 
 def conv_silu(above, own, below, weight, bias, blocks):
     frames, height, cols, channels = own.shape
-    edge = pl.BlockSpec(above.shape, lambda s: (0, 0, 0, 0))
+    whole = pl.BlockSpec(memory_space=pltpu.VMEM)
     out_shape = (blocks, frames, height, cols // blocks, channels)
     return pl.pallas_call(
         conv_kernel,
         grid=(3,),
         in_specs=[
-            edge,
-            pl.BlockSpec(own.shape, lambda s: (0, 0, 0, 0)),
-            edge,
+            whole,
+            whole,
+            whole,
             pl.BlockSpec((3, 1, channels, channels), lambda s: (0, s, 0, 0)),
-            pl.BlockSpec((1, channels), lambda s: (0, 0)),
+            whole,
         ],
         out_specs=pl.BlockSpec(out_shape, lambda s: (0, 0, 0, 0, 0)),
         out_shape=jax.ShapeDtypeStruct(out_shape, BF16),
@@ -135,11 +135,12 @@
         grid=(rows,),
         in_specs=[
             spec,
-            pl.BlockSpec(wqkv.shape, lambda r: (0, 0)),
-            pl.BlockSpec(wo.shape, lambda r: (0, 0)),
+            pl.BlockSpec(memory_space=pltpu.VMEM),
+            pl.BlockSpec(memory_space=pltpu.VMEM),
         ],
         out_specs=spec,
         out_shape=jax.ShapeDtypeStruct(blocked.shape, BF16),
+        compiler_params=pltpu.CompilerParams(vmem_limit_bytes=24 * 2**20),
         cost_estimate=pl.CostEstimate(flops=5 * 10**9, bytes_accessed=4 * 10**6, transcendentals=0),
         name="attend",
     )(blocked, wqkv, wo)
@@ -186,7 +187,7 @@
         in_specs=[whole] * 8,
         out_specs=whole,
         out_shape=jax.ShapeDtypeStruct(out_shape, BF16),
-        compiler_params=pltpu.CompilerParams(vmem_limit_bytes=40 * 2**20),
+        compiler_params=pltpu.CompilerParams(vmem_limit_bytes=32 * 2**20),
         cost_estimate=pl.CostEstimate(flops=5 * 10**9, bytes_accessed=8 * 10**6, transcendentals=0),
         name="kernel_grad",
     )(*cots, *mixes)

time: 166 us -> 168 us (1.012)
  blocking collectives: 69.3 us -> 62.4 us
  waiting for transfers between devices: 21 us -> 27.4 us
  local copies, waits for them, and re-layouts: 6.78 us -> 11.7 us
  Pallas kernels: 23.7 us -> 21.4 us
    all_to_all x1, waiting for transfers between devices: 7.4 us -> 12.4 us  [on_device(): blocked = lax.all_to_all(hidden, FRAME, 0, 0, tiled=True)]
    all_to_all x1, blocking collectives: 31.8 us -> 27.1 us  [on_device(): back = lax.all_to_all(sent, FRAME, 0, 0, tiled=True)]
    unnamed x18 -> x24, local copies, waits for them, and re-layouts: 1.77 us -> 5.15 us
    pallas_call x1, Pallas kernels: 8.65 us -> 6.42 us  [attend(): pl.pallas_call(attention_kernel, grid=(rows,), in_specs=[spec, pl.BlockSp...]
    all_to_all x1, blocking collectives: 37.5 us -> 35.3 us  [sum_over_devices(): lax.all_to_all(partial.reshape(nx * ny, rows, width), ('x', 'y'), 0, 0, t...]
  transfers between devices with their start and end apart: 10 -> 10, of which waited for: 5 -> 5; matrix products, arithmetic and copies ran while one was open for 7% -> 8% of each run, Pallas kernels for 6% -> 6%
where the time goes in v3:
time: 168 us; the launch traced here: 167 us
  blocking collectives  62.4 us (37%)
  starting transfers between devices  35.8 us (21%)
  waiting for transfers between devices  27.4 us (16%)
  Pallas kernels  21.4 us (13%)
  local copies, waits for them, and re-layouts  11.7 us (7%)
  matrix products  6.48 us (4%)
    all_to_all x1, blocking collectives, sum_over_devices(): lax.all_to_all(partial.reshape(nx * ny, rows, width), ('x', 'y'), 0, 0, t...  35.3 us
    all_to_all x1, blocking collectives, on_device(): back = lax.all_to_all(sent, FRAME, 0, 0, tiled=True)  27.1 us
    ppermute x2, starting transfers between devices, edge_rows(): below = lax.ppermute(head, TILE, [(i + 1, i) for i in range(count - 1)])  12.7 us
    all_to_all x1, waiting for transfers between devices, on_device(): blocked = lax.all_to_all(hidden, FRAME, 0, 0, tiled=True)  12.4 us
    all_to_all x1, starting transfers between devices, on_device(): blocked = lax.all_to_all(hidden, FRAME, 0, 0, tiled=True)  10.9 us
    pallas_call x1, Pallas kernels, conv_silu(): pl.pallas_call(conv_kernel, grid=(3,), in_specs=[whole, whole, whole, pl....  9.95 us
    all_to_all x1, waiting for transfers between devices, sum_over_devices(): part = lax.all_to_all(part, ('zh', 'zl'), 0, 0, tiled=True)  8.37 us
    all_to_all x1, starting transfers between devices, sum_over_devices(): part = lax.all_to_all(part, ('zh', 'zl'), 0, 0, tiled=True)  7.61 us
  transfers between devices with their start and end apart: 10, of which 5 were waited for; matrix products, arithmetic and copies ran while one was open for 8% of the time, Pallas kernels for 6%

profile of v3, /device:TPU:8, one launch (start us, length us, event | category | flops | bytes accessed | tf_op | source)
XLA Modules:
  0.0 167.2 jit_solution(17429819981836756706)
XLA Ops:
  0.7 2.0 %fusion.18 = (bf16[2,1,128,512]{3,2,1,0:T(8,128)(2,1)}, bf16[2,1,128,512]{3,2,1,0:T(8,128)(2,1)}) fusion(bf16[2,4,128,512]{3,2,1,0:T(8,128)(2,1)} %param.15), kind=kLoop, calls=%fused_computation.35 | loop fusion | bytes 1048576 | tf_op jit(solution)/shard_map/slice | solution.py:21
  2.6 1.9 %collective-permute-start.2 = (bf16[2,1,128,512]{3,2,1,0:T(8,128)(2,1)}, bf16[2,1,128,512]{3,2,1,0:T(8,128)(2,1)}, u32[]{:S(2)}, u32[]{:S(2)}) collective-permute-start(bf16[2,1,128,512]{3,2,1,0:T(8,128)(2,1)} %get-tuple-element.21), channel_id=1, source_target_pairs={{0,1},{1,2},{2,3},{3,4},{4,5},{5,6},{6,7},{7,8},{8,9},{9,10},{10,1... | collective-permute-start | bytes 786440 | tf_op jit(solution)/shard_map/ppermute | solution.py:23
  4.6 6.3 %collective-permute-start.3 = (bf16[2,1,128,512]{3,2,1,0:T(8,128)(2,1)}, bf16[2,1,128,512]{3,2,1,0:T(8,128)(2,1)S(1)}, u32[]{:S(2)}, u32[]{:S(2)}) collective-permute-start(bf16[2,1,128,512]{3,2,1,0:T(8,128)(2,1)} %get-tuple-element.20), channel_id=1, source_target_pairs={{1,0},{2,1},{3,2},{4,3},{5,4},{6,5},{7,6},{8,7},{9,8},{10,9},{11,1... | collective-permute-start | bytes 786440 | tf_op jit(solution)/shard_map/ppermute | solution.py:24
  10.9 1.9 %fusion.19 = (bf16[2,1,128,512]{3,2,1,0:T(8,128)(2,1)}, bf16[2,1,128,512]{3,2,1,0:T(8,128)(2,1)}) fusion(bf16[2,4,128,512]{3,2,1,0:T(8,128)(2,1)} %own_ref.1), kind=kLoop, calls=%fused_computation.36 | loop fusion | bytes 1048576 | tf_op jit(solution)/shard_map/slice | solution.py:21
  12.8 1.9 %collective-permute-start = (bf16[2,1,128,512]{3,2,1,0:T(8,128)(2,1)}, bf16[2,1,128,512]{3,2,1,0:T(8,128)(2,1)}, u32[]{:S(2)}, u32[]{:S(2)}) collective-permute-start(bf16[2,1,128,512]{3,2,1,0:T(8,128)(2,1)} %get-tuple-element.23), channel_id=1, source_target_pairs={{0,1},{1,2},{2,3},{3,4},{4,5},{5,6},{6,7},{7,8},{8,9},{9,10},{10,1... | collective-permute-start | bytes 786440 | tf_op jit(solution)/shard_map/ppermute | solution.py:23
  14.7 6.3 %collective-permute-start.1 = (bf16[2,1,128,512]{3,2,1,0:T(8,128)(2,1)}, bf16[2,1,128,512]{3,2,1,0:T(8,128)(2,1)}, u32[]{:S(2)}, u32[]{:S(2)}) collective-permute-start(bf16[2,1,128,512]{3,2,1,0:T(8,128)(2,1)} %get-tuple-element.22), channel_id=1, source_target_pairs={{1,0},{2,1},{3,2},{4,3},{5,4},{6,5},{7,6},{8,7},{9,8},{10,9},{11,1... | collective-permute-start | bytes 786440 | tf_op jit(solution)/shard_map/ppermute | solution.py:24
  21.2 3.8 %collective-permute-done.above_ref = bf16[2,1,128,512]{3,2,1,0:T(8,128)(2,1)} collective-permute-done((bf16[2,1,128,512]{3,2,1,0:T(8,128)(2,1)}, bf16[2,1,128,512]{3,2,1,0:T(8,128)(2,1)}, u32[]{:S(2)}, u32[]{:S(2)}) %collective-permute-start) | collective-permute-done | bytes 262176 | tf_op jit(solution)/shard_map/ppermute | solution.py:23
  25.2 10.0 %conv_silu.1 = bf16[8,2,4,16,512]{4,3,2,1,0:T(8,128)(2,1)} custom-call(bf16[2,1,128,512]{3,2,1,0:T(8,128)(2,1)} %collective-permute-done.above_ref, bf16[2,4,128,512]{3,2,1,0:T(8,128)(2,1)} %own_ref.1, bf16[2,1,128,512]{3,2,1,0:T(8,128)(2,1)} %collective-permute-done.1.below_ref, bf16[3,3,512,512]{3,2,1,0:T(8,128)(2,1)} %weight_ref.1, f32[1,512]{1,0:T(1,128)} %bitcast.29), custom_call_target="tpu_custom_call" | custom-call | flops 5000000000 | bytes 8000000 | tf_op jit(solution)/shard_map/conv_silu/pallas_call | solution.py:72
  35.2 10.9 %all-to-all-start = ((bf16[8,2,4,16,512]{4,3,2,1,0:T(8,128)(2,1)}), bf16[8,2,4,16,512]{4,3,2,1,0:T(8,128)(2,1)S(1)}, u32[]{:S(2)}, u32[]{:S(2)}) async-start(bf16[8,2,4,16,512]{4,3,2,1,0:T(8,128)(2,1)} %conv_silu.1), calls=%async_computation | async-start | bytes 2097152 | tf_op jit(solution)/shard_map/all_to_all | solution.py:238
  46.1 1.0 constant_dynamic-update-slice_fusion.2
  47.1 1.3 constant_dynamic-update-slice_fusion.1
  51.9 1.5 convolution_convert_fusion.3.refs_2_
  53.5 1.5 convolution_convert_fusion.5.refs_0_
  55.0 1.6 convolution_convert_fusion.4.refs_1_
  58.3 12.4 %all-to-all-done = bf16[8,2,4,16,512]{4,3,2,1,0:T(8,128)(2,1)S(1)} async-done(((bf16[8,2,4,16,512]{4,3,2,1,0:T(8,128)(2,1)}), bf16[8,2,4,16,512]{4,3,2,1,0:T(8,128)(2,1)S(1)}, u32[]{:S(2)}, u32[]{:S(2)}) %all-to-all-start) | async-done | bytes 1048608 | tf_op jit(solution)/shard_map/all_to_all | solution.py:238
  70.7 1.0 copy-done.4
  71.7 6.4 %attend.1 = bf16[16,4,16,512]{3,2,1,0:T(8,128)(2,1)S(1)} custom-call(bf16[16,4,16,512]{3,2,1,0:T(8,128)(2,1)S(1)} %bitcast.19, bf16[512,1536]{1,0:T(8,128)(2,1)S(1)} %pad_maximum_fusion.wqkv_ref, bf16[512,512]{1,0:T(8,128)(2,1)S(1)} %copy-done.4), custom_call_target="tpu_custom_call" | custom-call | flops 5000000000 | bytes 4000000 | tf_op jit(solution)/shard_map/attend/pallas_call | solution.py:133
  78.2 27.1 %all_to_all.20.refs_6_ = bf16[8,2,4,16,512]{4,3,2,1,0:T(8,128)(2,1)S(1)} all-to-all(bf16[8,2,4,16,512]{4,3,2,1,0:T(8,128)(2,1)S(1)} %bitcast.20), channel_id=1, replica_groups=mesh['zh'=2,'x'=4,'y'=4,'zl'=4,'core'=2] {'zh','x'}, dimensions={0} | all-to-all | bytes 2097152 | tf_op jit(solution)/shard_map/all_to_all | solution.py:244
  105.3 2.7 %collective-permute-done.7.refs_7_ = bf16[8,2,4,16,512]{4,3,2,1,0:T(8,128)(2,1)S(1)} collective-permute-done((bf16[8,2,4,16,512]{4,3,2,1,0:T(8,128)(2,1)S(1)}, bf16[8,2,4,16,512]{4,3,2,1,0:T(8,128)(2,1)S(1)}, u32[]{:S(2)}, u32[]{:S(2)}) %collective-permute-start.7) | collective-permute-done | bytes 1048608 | tf_op jit(solution)/shard_map/ppermute | solution.py:197
  108.0 5.1 %kernel_grad.1 = bf16[4,256,1152]{2,1,0:T(8,128)(2,1)S(1)} custom-call(bf16[256,1536]{1,0:T(8,128)(2,1)S(1)} %copy-done.6, bf16[256,1536]{1,0:T(8,128)(2,1)S(1)} %copy-done.7, bf16[256,1536]{1,0:T(8,128)(2,1)S(1)} %copy-done.5, bf16[256,1536]{1,0:T(8,128)(2,1)S(1)} %collective-permute-done.4.refs_3_, bf16[256,1536]{1,0:T(8,128)(2,1)S(1)} %copy-done.3, ...), custom_call_target="tpu_custom_call" | custom-call | flops 5000000000 | bytes 8000000 | tf_op jit(solution)/shard_map/kernel_grad/pallas_call | solution.py:185
  113.1 35.3 %all_to_all.21 = bf16[16,64,1152]{2,1,0:T(8,128)(2,1)S(1)} all-to-all(bf16[16,64,1152]{2,1,0:T(8,128)(2,1)S(1)} %bitcast.18), channel_id=1, replica_groups=mesh['zh'=2,'x'=4,'y'=4,'zl'=4,'core'=2] {'x','y'}, dimensions={0} | all-to-all | bytes 4718592 | tf_op jit(solution)/shard_map/all_to_all | solution.py:223
  149.6 7.6 %all-to-all-start.3 = ((bf16[8,16,576]{2,1,0:T(8,128)(2,1)}), bf16[8,16,576]{2,1,0:T(8,128)(2,1)S(1)}, u32[]{:S(2)}, u32[]{:S(2)}) async-start(bf16[8,16,576]{2,1,0:T(8,128)(2,1)} %bitcast.10), calls=%async_computation.3 | async-start | bytes 327680 | tf_op jit(solution)/shard_map/all_to_all | solution.py:227
  157.2 1.1 copy.11
  158.2 8.4 %all-to-all-done.3 = bf16[8,16,576]{2,1,0:T(8,128)(2,1)S(1)} async-done(((bf16[8,16,576]{2,1,0:T(8,128)(2,1)}), bf16[8,16,576]{2,1,0:T(8,128)(2,1)S(1)}, u32[]{:S(2)}, u32[]{:S(2)}) %all-to-all-start.3) | async-done | bytes 147488 | tf_op jit(solution)/shard_map/all_to_all | solution.py:227
  (44 shorter events, 7.4 us)
Async XLA Ops:
  0.6 20.4 %copy-start.10 = (bf16[512,512]{1,0:T(8,128)(2,1)S(1)}, bf16[512,512]{1,0:T(8,128)(2,1)}, u32[]{:S(2)}) copy-start(bf16[512,512]{1,0:T(8,128)(2,1)} %param.11) | copy-start | bytes 1572868
  0.6 20.4 %copy-start.9 = (bf16[512,512]{1,0:T(8,128)(2,1)S(1)}, bf16[512,512]{1,0:T(8,128)(2,1)}, u32[]{:S(2)}) copy-start(bf16[512,512]{1,0:T(8,128)(2,1)} %param.12) | copy-start | bytes 1572868
  0.7 20.4 %copy-start.8 = (bf16[512,512]{1,0:T(8,128)(2,1)S(1)}, bf16[512,512]{1,0:T(8,128)(2,1)}, u32[]{:S(2)}) copy-start(bf16[512,512]{1,0:T(8,128)(2,1)} %param.13) | copy-start | bytes 1572868
  2.6 43.5 %collective-permute-start.2 = (bf16[2,1,128,512]{3,2,1,0:T(8,128)(2,1)}, bf16[2,1,128,512]{3,2,1,0:T(8,128)(2,1)}, u32[]{:S(2)}, u32[]{:S(2)}) collective-permute-start(bf16[2,1,128,512]{3,2,1,0:T(8,128)(2,1)} %get-tuple-element.21), channel_id=1, source_target_pairs={{0,1},{1,2},{2,3},{3,4},{4,5},{5,6},{6,7},{7,8},{8,9},{9,10},{10,1... | collective-permute-start | bytes 786440 | tf_op jit(solution)/shard_map/ppermute | solution.py:23
  4.6 43.8 %collective-permute-start.3 = (bf16[2,1,128,512]{3,2,1,0:T(8,128)(2,1)}, bf16[2,1,128,512]{3,2,1,0:T(8,128)(2,1)S(1)}, u32[]{:S(2)}, u32[]{:S(2)}) collective-permute-start(bf16[2,1,128,512]{3,2,1,0:T(8,128)(2,1)} %get-tuple-element.20), channel_id=1, source_target_pairs={{1,0},{2,1},{3,2},{4,3},{5,4},{6,5},{7,6},{8,7},{9,8},{10,9},{11,1... | collective-permute-start | bytes 786440 | tf_op jit(solution)/shard_map/ppermute | solution.py:24
  12.8 12.3 %collective-permute-start = (bf16[2,1,128,512]{3,2,1,0:T(8,128)(2,1)}, bf16[2,1,128,512]{3,2,1,0:T(8,128)(2,1)}, u32[]{:S(2)}, u32[]{:S(2)}) collective-permute-start(bf16[2,1,128,512]{3,2,1,0:T(8,128)(2,1)} %get-tuple-element.23), channel_id=1, source_target_pairs={{0,1},{1,2},{2,3},{3,4},{4,5},{5,6},{6,7},{7,8},{8,9},{9,10},{10,1... | collective-permute-start | bytes 786440 | tf_op jit(solution)/shard_map/ppermute | solution.py:23
  14.7 10.5 %collective-permute-start.1 = (bf16[2,1,128,512]{3,2,1,0:T(8,128)(2,1)}, bf16[2,1,128,512]{3,2,1,0:T(8,128)(2,1)}, u32[]{:S(2)}, u32[]{:S(2)}) collective-permute-start(bf16[2,1,128,512]{3,2,1,0:T(8,128)(2,1)} %get-tuple-element.22), channel_id=1, source_target_pairs={{1,0},{2,1},{3,2},{4,3},{5,4},{6,5},{7,6},{8,7},{9,8},{10,9},{11,1... | collective-permute-start | bytes 786440 | tf_op jit(solution)/shard_map/ppermute | solution.py:24
  35.2 35.5 %all-to-all-start = ((bf16[8,2,4,16,512]{4,3,2,1,0:T(8,128)(2,1)}), bf16[8,2,4,16,512]{4,3,2,1,0:T(8,128)(2,1)S(1)}, u32[]{:S(2)}, u32[]{:S(2)}) async-start(bf16[8,2,4,16,512]{4,3,2,1,0:T(8,128)(2,1)} %conv_silu.1), calls=%async_computation | async-start | bytes 2097152 | tf_op jit(solution)/shard_map/all_to_all | solution.py:238
  49.9 6.7 %collective-permute-start.4 = (bf16[256,1536]{1,0:T(8,128)(2,1)S(1)}, bf16[256,1536]{1,0:T(8,128)(2,1)S(1)}, u32[]{:S(2)}, u32[]{:S(2)}) collective-permute-start(bf16[256,1536]{1,0:T(8,128)(2,1)S(1)} %convolution_convert_fusion.2), channel_id=1, source_target_pairs={{0,1},{1,0},{2,3},{3,2},{4,5},{5,4},{6,7},{7,6},{8,9},{9,8},{10,11... | collective-permute-start | bytes 2359304 | tf_op jit(solution)/shard_map/ppermute | solution.py:197
  50.6 5.9 %collective-permute-start.6 = (bf16[256,1536]{1,0:T(8,128)(2,1)S(1)}, bf16[256,1536]{1,0:T(8,128)(2,1)S(1)}, u32[]{:S(2)}, u32[]{:S(2)}) collective-permute-start(bf16[256,1536]{1,0:T(8,128)(2,1)S(1)} %convolution_convert_fusion), channel_id=1, source_target_pairs={{0,1},{1,0},{2,3},{3,2},{4,5},{5,4},{6,7},{7,6},{8,9},{9,8},{10,11... | collective-permute-start | bytes 2359304 | tf_op jit(solution)/shard_map/ppermute | solution.py:197
  51.8 5.6 %collective-permute-start.5 = (bf16[256,1536]{1,0:T(8,128)(2,1)S(1)}, bf16[256,1536]{1,0:T(8,128)(2,1)S(1)}, u32[]{:S(2)}, u32[]{:S(2)}) collective-permute-start(bf16[256,1536]{1,0:T(8,128)(2,1)S(1)} %convolution_convert_fusion.1), channel_id=1, source_target_pairs={{0,1},{1,0},{2,3},{3,2},{4,5},{5,4},{6,7},{7,6},{8,9},{9,8},{10,11... | collective-permute-start | bytes 2359304 | tf_op jit(solution)/shard_map/ppermute | solution.py:197
  56.5 0.9 copy-start
  57.4 0.9 copy-start.2
  70.7 1.0 copy-start.4
  71.7 36.2 %copy-start.5 = (bf16[256,1536]{1,0:T(8,128)(2,1)S(1)}, bf16[256,1536]{1,0:T(8,128)(2,1)}, u32[]{:S(2)}) copy-start(bf16[256,1536]{1,0:T(8,128)(2,1)} %convolution_convert_fusion.3.refs_2_) | copy-start | bytes 2359300
  71.7 36.2 %copy-start.6 = (bf16[256,1536]{1,0:T(8,128)(2,1)S(1)}, bf16[256,1536]{1,0:T(8,128)(2,1)}, u32[]{:S(2)}) copy-start(bf16[256,1536]{1,0:T(8,128)(2,1)} %convolution_convert_fusion.5.refs_0_) | copy-start | bytes 2359300
  71.7 36.2 %copy-start.7 = (bf16[256,1536]{1,0:T(8,128)(2,1)S(1)}, bf16[256,1536]{1,0:T(8,128)(2,1)}, u32[]{:S(2)}) copy-start(bf16[256,1536]{1,0:T(8,128)(2,1)} %convolution_convert_fusion.4.refs_1_) | copy-start | bytes 2359300
  78.2 29.8 %copy-start.1 = (bf16[256,1536]{1,0:T(8,128)(2,1)S(1)}, bf16[256,1536]{1,0:T(8,128)(2,1)}, u32[]{:S(2)}) copy-start(bf16[256,1536]{1,0:T(8,128)(2,1)} %copy-done) | copy-start | bytes 2359300
  78.2 29.8 %copy-start.3 = (bf16[256,1536]{1,0:T(8,128)(2,1)S(1)}, bf16[256,1536]{1,0:T(8,128)(2,1)}, u32[]{:S(2)}) copy-start(bf16[256,1536]{1,0:T(8,128)(2,1)} %copy-done.2) | copy-start | bytes 2359300
  105.3 2.7 %collective-permute-start.7 = (bf16[8,2,4,16,512]{4,3,2,1,0:T(8,128)(2,1)S(1)}, bf16[8,2,4,16,512]{4,3,2,1,0:T(8,128)(2,1)S(1)}, u32[]{:S(2)}, u32[]{:S(2)}) collective-permute-start(bf16[8,2,4,16,512]{4,3,2,1,0:T(8,128)(2,1)S(1)} %all_to_all.20.refs_6_), channel_id=1, source_target_pairs={{0,1},{1,0},{2,3},{3,2},{4,5},{5,4},{6,7},{7,6},{8,9},{9,8},{10,11... | collective-permute-start | bytes 3145736 | tf_op jit(solution)/shard_map/ppermute | solution.py:197
  149.6 17.0 %all-to-all-start.3 = ((bf16[8,16,576]{2,1,0:T(8,128)(2,1)}), bf16[8,16,576]{2,1,0:T(8,128)(2,1)S(1)}, u32[]{:S(2)}, u32[]{:S(2)}) async-start(bf16[8,16,576]{2,1,0:T(8,128)(2,1)} %bitcast.10), calls=%async_computation.3 | async-start | bytes 327680 | tf_op jit(solution)/shard_map/all_to_all | solution.py:227

commit v4 on v3

--- a/solution.py
+++ b/solution.py
@@ -25,65 +25,56 @@
     return above, below
 
 
-def conv_kernel(above_ref, own_ref, below_ref, weight_ref, bias_ref, out_ref, rows_ref, acc_ref):
-    s = pl.program_id(0)
+def conv_kernel(
+    above_ref, own_ref, below_ref, weight_ref, bias_ref, out_ref, taps_ref, held_ref, in_sem, out_sem
+):
+    loads = []
+    for s in range(3):
+        loads.append(pltpu.make_async_copy(weight_ref.at[:, s], taps_ref.at[s], in_sem.at[s]))
+        loads[s].start()
     frames, height, cols, channels = own_ref.shape
     pixels = height * cols
-
-    @pl.when(s == 0)
-    def _():
-        for f in range(frames):
-            rows_ref[f, :cols] = above_ref[f, 0]
-            rows_ref[f, cols : cols + pixels] = own_ref[f].reshape(pixels, channels)
-            rows_ref[f, cols + pixels :] = below_ref[f, 0]
-
+    blocks = out_ref.shape[0]
     column = lax.broadcasted_iota(jnp.int32, (pixels, 1), 0) % cols
-    blocks = out_ref.shape[0]
+    stores = []
     for f in range(frames):
-        taps = [rows_ref[f, r * cols : r * cols + pixels] for r in range(3)]
-        part = jnp.dot(
-            jnp.concatenate(taps, axis=1),
-            weight_ref[...].reshape(3 * channels, channels),
-            preferred_element_type=F32,
-        )
-
-        @pl.when(s == 0)
-        def _():
-            acc_ref[f] = jnp.where(column > 0, pltpu.roll(part, 1, 0), 0.0)
-
-        @pl.when(s == 1)
-        def _():
-            acc_ref[f] += part
-
-        @pl.when(s == 2)
-        def _():
-            moved = jnp.where(column < cols - 1, pltpu.roll(part, pixels - 1, 0), 0.0)
-            v = acc_ref[f] + moved + bias_ref[...]
-            h = (v / (1.0 + jnp.exp(-v))).astype(BF16)
-            h = h.reshape(height, blocks, cols // blocks, channels)
-            for b in range(blocks):
-                out_ref[b, f] = h[:, b]
+        rows = [above_ref[f, 0]] + [own_ref[f, y] for y in range(height)] + [below_ref[f, 0]]
+        cells = [jnp.concatenate(rows[r : r + height], axis=0) for r in range(3)]
+        cells = jnp.concatenate(cells, axis=1)
+        parts = []
+        for s in range(3):
+            if f == 0:
+                loads[s].wait()
+            weight = taps_ref[s].reshape(3 * channels, channels)
+            parts.append(jnp.dot(cells, weight, preferred_element_type=F32))
+        left = jnp.where(column > 0, pltpu.roll(parts[0], 1, 0), 0.0)
+        right = jnp.where(column < cols - 1, pltpu.roll(parts[2], pixels - 1, 0), 0.0)
+        v = left + parts[1] + right + bias_ref[...]
+        h = (v / (1.0 + jnp.exp(-v))).astype(BF16)
+        h = h.reshape(height, blocks, cols // blocks, channels)
+        for b in range(blocks):
+            held_ref[f, b] = h[:, b]
+        stores.append(pltpu.make_async_copy(held_ref.at[f], out_ref.at[:, f], out_sem.at[f]))
+        stores[f].start()
+    for store in stores:
+        store.wait()
 
 
 def conv_silu(above, own, below, weight, bias, blocks):
     frames, height, cols, channels = own.shape
     whole = pl.BlockSpec(memory_space=pltpu.VMEM)
-    out_shape = (blocks, frames, height, cols // blocks, channels)
+    far = pl.BlockSpec(memory_space=pltpu.HBM)
+    width = cols // blocks
     return pl.pallas_call(
         conv_kernel,
-        grid=(3,),
-        in_specs=[
-            whole,
-            whole,
-            whole,
-            pl.BlockSpec((3, 1, channels, channels), lambda s: (0, s, 0, 0)),
-            whole,
-        ],
-        out_specs=pl.BlockSpec(out_shape, lambda s: (0, 0, 0, 0, 0)),
-        out_shape=jax.ShapeDtypeStruct(out_shape, BF16),
+        in_specs=[whole, whole, whole, far, whole],
+        out_specs=far,
+        out_shape=jax.ShapeDtypeStruct((blocks, frames, height, width, channels), BF16),
         scratch_shapes=[
-            pltpu.VMEM((frames, (height + 2) * cols, channels), BF16),
-            pltpu.VMEM((frames, height * cols, channels), F32),
+            pltpu.VMEM((3, 3, channels, channels), BF16),
+            pltpu.VMEM((frames, blocks, height, width, channels), BF16),
+            pltpu.SemaphoreType.DMA((3,)),
+            pltpu.SemaphoreType.DMA((frames,)),
         ],
         cost_estimate=pl.CostEstimate(flops=5 * 10**9, bytes_accessed=8 * 10**6, transcendentals=0),
         name="conv_silu",

time: 168 us -> 167 us (level)
  no operation moved by 1% of the time
where the time goes in v4:
time: 167 us
  blocking collectives  62.4 us (37%)
  starting transfers between devices  35.8 us (21%)
  waiting for transfers between devices  27.4 us (16%)
  Pallas kernels  21 us (13%)
  local copies, waits for them, and re-layouts  11.7 us (7%)
  matrix products  6.48 us (4%)
    all_to_all x1, blocking collectives, sum_over_devices(): lax.all_to_all(partial.reshape(nx * ny, rows, width), ('x', 'y'), 0, 0, t...  35.3 us
    all_to_all x1, blocking collectives, on_device(): back = lax.all_to_all(sent, FRAME, 0, 0, tiled=True)  27.1 us
    ppermute x2, starting transfers between devices, edge_rows(): below = lax.ppermute(head, TILE, [(i + 1, i) for i in range(count - 1)])  12.7 us
    all_to_all x1, waiting for transfers between devices, on_device(): blocked = lax.all_to_all(hidden, FRAME, 0, 0, tiled=True)  12.4 us
    all_to_all x1, starting transfers between devices, on_device(): blocked = lax.all_to_all(hidden, FRAME, 0, 0, tiled=True)  10.9 us
    pallas_call x1, Pallas kernels, conv_silu(): pl.pallas_call(conv_kernel, in_specs=[whole, whole, whole, far, whole], o...  9.51 us
    all_to_all x1, waiting for transfers between devices, sum_over_devices(): part = lax.all_to_all(part, ('zh', 'zl'), 0, 0, tiled=True)  8.37 us
    all_to_all x1, starting transfers between devices, sum_over_devices(): part = lax.all_to_all(part, ('zh', 'zl'), 0, 0, tiled=True)  7.6 us
  transfers between devices with their start and end apart: 10, of which 5 were waited for; matrix products, arithmetic and copies ran while one was open for 8% of the time, Pallas kernels for 6%

profile of v4, /device:TPU:8, one launch (start us, length us, event | category | flops | bytes accessed | tf_op | source)
XLA Modules:
  0.0 166.8 jit_solution(14954223150570197827)
XLA Ops:
  0.7 2.0 %fusion.18 = (bf16[2,1,128,512]{3,2,1,0:T(8,128)(2,1)}, bf16[2,1,128,512]{3,2,1,0:T(8,128)(2,1)}) fusion(bf16[2,4,128,512]{3,2,1,0:T(8,128)(2,1)} %param.15), kind=kLoop, calls=%fused_computation.35 | loop fusion | bytes 1048576 | tf_op jit(solution)/shard_map/slice | solution.py:21
  2.6 1.9 %collective-permute-start.2 = (bf16[2,1,128,512]{3,2,1,0:T(8,128)(2,1)}, bf16[2,1,128,512]{3,2,1,0:T(8,128)(2,1)}, u32[]{:S(2)}, u32[]{:S(2)}) collective-permute-start(bf16[2,1,128,512]{3,2,1,0:T(8,128)(2,1)} %get-tuple-element.21), channel_id=1, source_target_pairs={{0,1},{1,2},{2,3},{3,4},{4,5},{5,6},{6,7},{7,8},{8,9},{9,10},{10,1... | collective-permute-start | bytes 786440 | tf_op jit(solution)/shard_map/ppermute | solution.py:23
  4.6 6.3 %collective-permute-start.3 = (bf16[2,1,128,512]{3,2,1,0:T(8,128)(2,1)}, bf16[2,1,128,512]{3,2,1,0:T(8,128)(2,1)S(1)}, u32[]{:S(2)}, u32[]{:S(2)}) collective-permute-start(bf16[2,1,128,512]{3,2,1,0:T(8,128)(2,1)} %get-tuple-element.20), channel_id=1, source_target_pairs={{1,0},{2,1},{3,2},{4,3},{5,4},{6,5},{7,6},{8,7},{9,8},{10,9},{11,1... | collective-permute-start | bytes 786440 | tf_op jit(solution)/shard_map/ppermute | solution.py:24
  10.9 1.9 %fusion.19 = (bf16[2,1,128,512]{3,2,1,0:T(8,128)(2,1)}, bf16[2,1,128,512]{3,2,1,0:T(8,128)(2,1)}) fusion(bf16[2,4,128,512]{3,2,1,0:T(8,128)(2,1)} %own_ref.1), kind=kLoop, calls=%fused_computation.36 | loop fusion | bytes 1048576 | tf_op jit(solution)/shard_map/slice | solution.py:21
  12.8 1.9 %collective-permute-start = (bf16[2,1,128,512]{3,2,1,0:T(8,128)(2,1)}, bf16[2,1,128,512]{3,2,1,0:T(8,128)(2,1)}, u32[]{:S(2)}, u32[]{:S(2)}) collective-permute-start(bf16[2,1,128,512]{3,2,1,0:T(8,128)(2,1)} %get-tuple-element.23), channel_id=1, source_target_pairs={{0,1},{1,2},{2,3},{3,4},{4,5},{5,6},{6,7},{7,8},{8,9},{9,10},{10,1... | collective-permute-start | bytes 786440 | tf_op jit(solution)/shard_map/ppermute | solution.py:23
  14.7 6.3 %collective-permute-start.1 = (bf16[2,1,128,512]{3,2,1,0:T(8,128)(2,1)}, bf16[2,1,128,512]{3,2,1,0:T(8,128)(2,1)}, u32[]{:S(2)}, u32[]{:S(2)}) collective-permute-start(bf16[2,1,128,512]{3,2,1,0:T(8,128)(2,1)} %get-tuple-element.22), channel_id=1, source_target_pairs={{1,0},{2,1},{3,2},{4,3},{5,4},{6,5},{7,6},{8,7},{9,8},{10,9},{11,1... | collective-permute-start | bytes 786440 | tf_op jit(solution)/shard_map/ppermute | solution.py:24
  21.2 3.8 %collective-permute-done.above_ref = bf16[2,1,128,512]{3,2,1,0:T(8,128)(2,1)} collective-permute-done((bf16[2,1,128,512]{3,2,1,0:T(8,128)(2,1)}, bf16[2,1,128,512]{3,2,1,0:T(8,128)(2,1)}, u32[]{:S(2)}, u32[]{:S(2)}) %collective-permute-start) | collective-permute-done | bytes 262176 | tf_op jit(solution)/shard_map/ppermute | solution.py:23
  25.2 9.5 %conv_silu.1 = bf16[8,2,4,16,512]{4,3,2,1,0:T(8,128)(2,1)} custom-call(bf16[2,1,128,512]{3,2,1,0:T(8,128)(2,1)} %collective-permute-done.above_ref, bf16[2,4,128,512]{3,2,1,0:T(8,128)(2,1)} %own_ref.1, bf16[2,1,128,512]{3,2,1,0:T(8,128)(2,1)} %collective-permute-done.1.below_ref, bf16[3,3,512,512]{3,2,1,0:T(8,128)(2,1)} %weight_ref.1, f32[1,512]{1,0:T(1,128)} %bitcast.29), custom_call_target="tpu_custom_call" | custom-call | flops 5000000000 | bytes 8000000 | tf_op jit(solution)/shard_map/conv_silu/pallas_call | solution.py:68
  34.7 10.9 %all-to-all-start = ((bf16[8,2,4,16,512]{4,3,2,1,0:T(8,128)(2,1)}), bf16[8,2,4,16,512]{4,3,2,1,0:T(8,128)(2,1)S(1)}, u32[]{:S(2)}, u32[]{:S(2)}) async-start(bf16[8,2,4,16,512]{4,3,2,1,0:T(8,128)(2,1)} %conv_silu.1), calls=%async_computation | async-start | bytes 2097152 | tf_op jit(solution)/shard_map/all_to_all | solution.py:229
  45.7 1.0 constant_dynamic-update-slice_fusion.2
  46.6 1.3 constant_dynamic-update-slice_fusion.1
  51.5 1.5 convolution_convert_fusion.3.refs_2_
  53.0 1.5 convolution_convert_fusion.5.refs_0_
  54.6 1.6 convolution_convert_fusion.4.refs_1_
  57.9 12.4 %all-to-all-done = bf16[8,2,4,16,512]{4,3,2,1,0:T(8,128)(2,1)S(1)} async-done(((bf16[8,2,4,16,512]{4,3,2,1,0:T(8,128)(2,1)}), bf16[8,2,4,16,512]{4,3,2,1,0:T(8,128)(2,1)S(1)}, u32[]{:S(2)}, u32[]{:S(2)}) %all-to-all-start) | async-done | bytes 1048608 | tf_op jit(solution)/shard_map/all_to_all | solution.py:229
  70.3 1.0 copy-done.4
  71.3 6.4 %attend.1 = bf16[16,4,16,512]{3,2,1,0:T(8,128)(2,1)S(1)} custom-call(bf16[16,4,16,512]{3,2,1,0:T(8,128)(2,1)S(1)} %bitcast.19, bf16[512,1536]{1,0:T(8,128)(2,1)S(1)} %pad_maximum_fusion.wqkv_ref, bf16[512,512]{1,0:T(8,128)(2,1)S(1)} %copy-done.4), custom_call_target="tpu_custom_call" | custom-call | flops 5000000000 | bytes 4000000 | tf_op jit(solution)/shard_map/attend/pallas_call | solution.py:124
  77.8 27.1 %all_to_all.20.refs_6_ = bf16[8,2,4,16,512]{4,3,2,1,0:T(8,128)(2,1)S(1)} all-to-all(bf16[8,2,4,16,512]{4,3,2,1,0:T(8,128)(2,1)S(1)} %bitcast.20), channel_id=1, replica_groups=mesh['zh'=2,'x'=4,'y'=4,'zl'=4,'core'=2] {'zh','x'}, dimensions={0} | all-to-all | bytes 2097152 | tf_op jit(solution)/shard_map/all_to_all | solution.py:235
  104.9 2.7 %collective-permute-done.7.refs_7_ = bf16[8,2,4,16,512]{4,3,2,1,0:T(8,128)(2,1)S(1)} collective-permute-done((bf16[8,2,4,16,512]{4,3,2,1,0:T(8,128)(2,1)S(1)}, bf16[8,2,4,16,512]{4,3,2,1,0:T(8,128)(2,1)S(1)}, u32[]{:S(2)}, u32[]{:S(2)}) %collective-permute-start.7) | collective-permute-done | bytes 1048608 | tf_op jit(solution)/shard_map/ppermute | solution.py:188
  107.6 5.1 %kernel_grad.1 = bf16[4,256,1152]{2,1,0:T(8,128)(2,1)S(1)} custom-call(bf16[256,1536]{1,0:T(8,128)(2,1)S(1)} %copy-done.6, bf16[256,1536]{1,0:T(8,128)(2,1)S(1)} %copy-done.7, bf16[256,1536]{1,0:T(8,128)(2,1)S(1)} %copy-done.5, bf16[256,1536]{1,0:T(8,128)(2,1)S(1)} %collective-permute-done.4.refs_3_, bf16[256,1536]{1,0:T(8,128)(2,1)S(1)} %copy-done.3, ...), custom_call_target="tpu_custom_call" | custom-call | flops 5000000000 | bytes 8000000 | tf_op jit(solution)/shard_map/kernel_grad/pallas_call | solution.py:176
  112.7 35.3 %all_to_all.21 = bf16[16,64,1152]{2,1,0:T(8,128)(2,1)S(1)} all-to-all(bf16[16,64,1152]{2,1,0:T(8,128)(2,1)S(1)} %bitcast.18), channel_id=1, replica_groups=mesh['zh'=2,'x'=4,'y'=4,'zl'=4,'core'=2] {'x','y'}, dimensions={0} | all-to-all | bytes 4718592 | tf_op jit(solution)/shard_map/all_to_all | solution.py:214
  149.1 7.6 %all-to-all-start.3 = ((bf16[8,16,576]{2,1,0:T(8,128)(2,1)}), bf16[8,16,576]{2,1,0:T(8,128)(2,1)S(1)}, u32[]{:S(2)}, u32[]{:S(2)}) async-start(bf16[8,16,576]{2,1,0:T(8,128)(2,1)} %bitcast.10), calls=%async_computation.3 | async-start | bytes 327680 | tf_op jit(solution)/shard_map/all_to_all | solution.py:218
  156.7 1.1 copy.11
  157.8 8.4 %all-to-all-done.3 = bf16[8,16,576]{2,1,0:T(8,128)(2,1)S(1)} async-done(((bf16[8,16,576]{2,1,0:T(8,128)(2,1)}), bf16[8,16,576]{2,1,0:T(8,128)(2,1)S(1)}, u32[]{:S(2)}, u32[]{:S(2)}) %all-to-all-start.3) | async-done | bytes 147488 | tf_op jit(solution)/shard_map/all_to_all | solution.py:218
  (44 shorter events, 7.4 us)
Async XLA Ops:
  0.6 20.4 %copy-start.10 = (bf16[512,512]{1,0:T(8,128)(2,1)S(1)}, bf16[512,512]{1,0:T(8,128)(2,1)}, u32[]{:S(2)}) copy-start(bf16[512,512]{1,0:T(8,128)(2,1)} %param.11) | copy-start | bytes 1572868
  0.6 20.4 %copy-start.9 = (bf16[512,512]{1,0:T(8,128)(2,1)S(1)}, bf16[512,512]{1,0:T(8,128)(2,1)}, u32[]{:S(2)}) copy-start(bf16[512,512]{1,0:T(8,128)(2,1)} %param.12) | copy-start | bytes 1572868
  0.7 20.4 %copy-start.8 = (bf16[512,512]{1,0:T(8,128)(2,1)S(1)}, bf16[512,512]{1,0:T(8,128)(2,1)}, u32[]{:S(2)}) copy-start(bf16[512,512]{1,0:T(8,128)(2,1)} %param.13) | copy-start | bytes 1572868
  2.6 43.0 %collective-permute-start.2 = (bf16[2,1,128,512]{3,2,1,0:T(8,128)(2,1)}, bf16[2,1,128,512]{3,2,1,0:T(8,128)(2,1)}, u32[]{:S(2)}, u32[]{:S(2)}) collective-permute-start(bf16[2,1,128,512]{3,2,1,0:T(8,128)(2,1)} %get-tuple-element.21), channel_id=1, source_target_pairs={{0,1},{1,2},{2,3},{3,4},{4,5},{5,6},{6,7},{7,8},{8,9},{9,10},{10,1... | collective-permute-start | bytes 786440 | tf_op jit(solution)/shard_map/ppermute | solution.py:23
  4.6 43.4 %collective-permute-start.3 = (bf16[2,1,128,512]{3,2,1,0:T(8,128)(2,1)}, bf16[2,1,128,512]{3,2,1,0:T(8,128)(2,1)S(1)}, u32[]{:S(2)}, u32[]{:S(2)}) collective-permute-start(bf16[2,1,128,512]{3,2,1,0:T(8,128)(2,1)} %get-tuple-element.20), channel_id=1, source_target_pairs={{1,0},{2,1},{3,2},{4,3},{5,4},{6,5},{7,6},{8,7},{9,8},{10,9},{11,1... | collective-permute-start | bytes 786440 | tf_op jit(solution)/shard_map/ppermute | solution.py:24
  12.8 12.3 %collective-permute-start = (bf16[2,1,128,512]{3,2,1,0:T(8,128)(2,1)}, bf16[2,1,128,512]{3,2,1,0:T(8,128)(2,1)}, u32[]{:S(2)}, u32[]{:S(2)}) collective-permute-start(bf16[2,1,128,512]{3,2,1,0:T(8,128)(2,1)} %get-tuple-element.23), channel_id=1, source_target_pairs={{0,1},{1,2},{2,3},{3,4},{4,5},{5,6},{6,7},{7,8},{8,9},{9,10},{10,1... | collective-permute-start | bytes 786440 | tf_op jit(solution)/shard_map/ppermute | solution.py:23
  14.7 10.5 %collective-permute-start.1 = (bf16[2,1,128,512]{3,2,1,0:T(8,128)(2,1)}, bf16[2,1,128,512]{3,2,1,0:T(8,128)(2,1)}, u32[]{:S(2)}, u32[]{:S(2)}) collective-permute-start(bf16[2,1,128,512]{3,2,1,0:T(8,128)(2,1)} %get-tuple-element.22), channel_id=1, source_target_pairs={{1,0},{2,1},{3,2},{4,3},{5,4},{6,5},{7,6},{8,7},{9,8},{10,9},{11,1... | collective-permute-start | bytes 786440 | tf_op jit(solution)/shard_map/ppermute | solution.py:24
  34.7 35.5 %all-to-all-start = ((bf16[8,2,4,16,512]{4,3,2,1,0:T(8,128)(2,1)}), bf16[8,2,4,16,512]{4,3,2,1,0:T(8,128)(2,1)S(1)}, u32[]{:S(2)}, u32[]{:S(2)}) async-start(bf16[8,2,4,16,512]{4,3,2,1,0:T(8,128)(2,1)} %conv_silu.1), calls=%async_computation | async-start | bytes 2097152 | tf_op jit(solution)/shard_map/all_to_all | solution.py:229
  49.5 6.7 %collective-permute-start.4 = (bf16[256,1536]{1,0:T(8,128)(2,1)S(1)}, bf16[256,1536]{1,0:T(8,128)(2,1)S(1)}, u32[]{:S(2)}, u32[]{:S(2)}) collective-permute-start(bf16[256,1536]{1,0:T(8,128)(2,1)S(1)} %convolution_convert_fusion.2), channel_id=1, source_target_pairs={{0,1},{1,0},{2,3},{3,2},{4,5},{5,4},{6,7},{7,6},{8,9},{9,8},{10,11... | collective-permute-start | bytes 2359304 | tf_op jit(solution)/shard_map/ppermute | solution.py:188
  50.2 5.9 %collective-permute-start.6 = (bf16[256,1536]{1,0:T(8,128)(2,1)S(1)}, bf16[256,1536]{1,0:T(8,128)(2,1)S(1)}, u32[]{:S(2)}, u32[]{:S(2)}) collective-permute-start(bf16[256,1536]{1,0:T(8,128)(2,1)S(1)} %convolution_convert_fusion), channel_id=1, source_target_pairs={{0,1},{1,0},{2,3},{3,2},{4,5},{5,4},{6,7},{7,6},{8,9},{9,8},{10,11... | collective-permute-start | bytes 2359304 | tf_op jit(solution)/shard_map/ppermute | solution.py:188
  51.4 5.6 %collective-permute-start.5 = (bf16[256,1536]{1,0:T(8,128)(2,1)S(1)}, bf16[256,1536]{1,0:T(8,128)(2,1)S(1)}, u32[]{:S(2)}, u32[]{:S(2)}) collective-permute-start(bf16[256,1536]{1,0:T(8,128)(2,1)S(1)} %convolution_convert_fusion.1), channel_id=1, source_target_pairs={{0,1},{1,0},{2,3},{3,2},{4,5},{5,4},{6,7},{7,6},{8,9},{9,8},{10,11... | collective-permute-start | bytes 2359304 | tf_op jit(solution)/shard_map/ppermute | solution.py:188
  56.1 0.9 copy-start
  57.0 0.9 copy-start.2
  70.3 1.0 copy-start.4
  71.3 36.2 %copy-start.5 = (bf16[256,1536]{1,0:T(8,128)(2,1)S(1)}, bf16[256,1536]{1,0:T(8,128)(2,1)}, u32[]{:S(2)}) copy-start(bf16[256,1536]{1,0:T(8,128)(2,1)} %convolution_convert_fusion.3.refs_2_) | copy-start | bytes 2359300
  71.3 36.2 %copy-start.6 = (bf16[256,1536]{1,0:T(8,128)(2,1)S(1)}, bf16[256,1536]{1,0:T(8,128)(2,1)}, u32[]{:S(2)}) copy-start(bf16[256,1536]{1,0:T(8,128)(2,1)} %convolution_convert_fusion.5.refs_0_) | copy-start | bytes 2359300
  71.3 36.2 %copy-start.7 = (bf16[256,1536]{1,0:T(8,128)(2,1)S(1)}, bf16[256,1536]{1,0:T(8,128)(2,1)}, u32[]{:S(2)}) copy-start(bf16[256,1536]{1,0:T(8,128)(2,1)} %convolution_convert_fusion.4.refs_1_) | copy-start | bytes 2359300
  77.8 29.8 %copy-start.1 = (bf16[256,1536]{1,0:T(8,128)(2,1)S(1)}, bf16[256,1536]{1,0:T(8,128)(2,1)}, u32[]{:S(2)}) copy-start(bf16[256,1536]{1,0:T(8,128)(2,1)} %copy-done) | copy-start | bytes 2359300
  77.8 29.8 %copy-start.3 = (bf16[256,1536]{1,0:T(8,128)(2,1)S(1)}, bf16[256,1536]{1,0:T(8,128)(2,1)}, u32[]{:S(2)}) copy-start(bf16[256,1536]{1,0:T(8,128)(2,1)} %copy-done.2) | copy-start | bytes 2359300
  104.9 2.7 %collective-permute-start.7 = (bf16[8,2,4,16,512]{4,3,2,1,0:T(8,128)(2,1)S(1)}, bf16[8,2,4,16,512]{4,3,2,1,0:T(8,128)(2,1)S(1)}, u32[]{:S(2)}, u32[]{:S(2)}) collective-permute-start(bf16[8,2,4,16,512]{4,3,2,1,0:T(8,128)(2,1)S(1)} %all_to_all.20.refs_6_), channel_id=1, source_target_pairs={{0,1},{1,0},{2,3},{3,2},{4,5},{5,4},{6,7},{7,6},{8,9},{9,8},{10,11... | collective-permute-start | bytes 3145736 | tf_op jit(solution)/shard_map/ppermute | solution.py:188
  149.1 17.0 %all-to-all-start.3 = ((bf16[8,16,576]{2,1,0:T(8,128)(2,1)}), bf16[8,16,576]{2,1,0:T(8,128)(2,1)S(1)}, u32[]{:S(2)}, u32[]{:S(2)}) async-start(bf16[8,16,576]{2,1,0:T(8,128)(2,1)} %bitcast.10), calls=%async_computation.3 | async-start | bytes 327680 | tf_op jit(solution)/shard_map/all_to_all | solution.py:218
